TPU v7x, 32 devices: a whole 2x2x4 slice. The times are simulated.
32 devices in a mesh: gx: 4 (over x, core), gy: 2 (over y), gz: 4 (over z).
Axes of the slice: x: 2, y: 2, z: 4, core: 2. Of those that a mesh axis runs over, the one named last changes fastest.
Arguments:
- opening_warmth_field: float32 [32, 32, 512], P('gx', 'gy', 'gz'), may hold values from -42 to 42
- cellwise_warming_source: float32 [32, 32, 512], P('gx', 'gy', 'gz'), may hold values from -6 to 6
- substance_category_per_voxel: int32 [32, 32, 512], P('gx', 'gy', 'gz'), may hold values from 0 to 15
- thermal_coefficient_table: float32 [16], replicated, may hold values from 0.2 to 5
- boundary_cooling_flags: int32 [32, 32, 512], P('gx', 'gy', 'gz'), may hold values 0 or 1
Outputs:
- closing_warmth_field: float32 [32, 32, 512], P('gx', 'gy', 'gz')
- remaining_mismatch: float32 [32, 32, 512], P('gx', 'gy', 'gz')
All inputs are finite; a program needn't handle non-finite values. No bound on the sum of `boundary_cooling_flags` on one device may be relied on, other than what follows from the above.
Results may differ from a plain program's by a relative error of at most 0.00055.
Values sent between devices are 32-bit elements; how exact they have to be, the bound alone decides.
A program may use at most 64 MiB of HBM per device.

v0:
```python
import functools

import jax
import jax.numpy as jnp
from jax import lax
from jax.experimental import pallas as pl
from jax.experimental.pallas import tpu as pltpu
from jax.sharding import PartitionSpec as P

ITERS = 4
interval_delta = 2.0
cooling = 3.0

MESH = pl.DeviceIdType.MESH
AXES = ("gx", "gy", "gz")
SUB = 8
DIRECT = 64
LANES = 128
FIELDS = 4
WARM, COND, SOURCE, FLAGS, EDGES = range(5)
SLOT = LANES // FIELDS
PAIRS = [(i, j) for i in range(ITERS + 1) for j in range(i, ITERS + 1) if i < ITERS]


def smooth(values, axis):
    size = values.shape[axis]
    return (values + values) + (pltpu.roll(values, 1, axis) + pltpu.roll(values, size - 1, axis))


def smooth_all(before, center, after):
    return smooth(smooth(before + (center + center) + after, 0), 1)


def kernel(
    counts,
    warm_in,
    source_in,
    category_in,
    table_in,
    flags_in,
    both_out,
    grid,
    basis,
    flux,
    warm_flux,
    diag,
    couple,
    table,
    table_row,
    ints,
    edges,
    mixed,
    beside,
    row_out,
    plane_rows,
    line_rows,
    all_rows,
    load_sems,
    raw_send,
    raw_recv,
    mix_send,
    mix_recv,
    fwd_send,
    fwd_recv,
    z_send,
    z_recv,
    row_send,
    row_recv,
):
    plane, line = counts[0] * counts[1], counts[2]
    nx, ny, nz = both_out.shape[1:]
    depth = ITERS + 1
    wide, tall, long = grid.shape[1:]
    short = ny + SUB
    here = [lax.axis_index(a) for a in AXES]
    in_plane = here[0] * counts[1] + here[1]
    plane_targets = [
        {"gx": other // counts[1], "gy": other % counts[1], "gz": here[2]}
        for other in [(in_plane + step) % plane for step in range(1, plane)]
    ]
    line_targets = [
        {"gx": here[0], "gy": here[1], "gz": (here[2] + step) % line} for step in range(1, line)
    ]

    loads = [
        pltpu.make_async_copy(category_in, ints.at[0], load_sems.at[0]),
        pltpu.make_async_copy(flags_in, ints.at[1], load_sems.at[1]),
        pltpu.make_async_copy(
            warm_in, grid.at[WARM, pl.ds(depth, nx), pl.ds(0, ny), pl.ds(0, nz)], load_sems.at[2]
        ),
        pltpu.make_async_copy(
            source_in, grid.at[SOURCE, pl.ds(depth, nx), pl.ds(0, ny), pl.ds(0, nz)], load_sems.at[3]
        ),
        pltpu.make_async_copy(table_in, table_row, load_sems.at[4]),
    ]
    for load in loads:
        load.start()

    for f in range(FIELDS + 1):
        grid[f, 0:depth, :, 0:nz] = jnp.zeros((depth, tall, nz), jnp.float32)
        grid[f, depth + nx :, :, 0:nz] = jnp.zeros((depth, tall, nz), jnp.float32)
        grid[f, depth : depth + nx, ny:, 0:nz] = jnp.zeros((nx, tall - ny, nz), jnp.float32)
    beside[...] = jnp.zeros(beside.shape, jnp.float32)
    table[...] = jnp.zeros(table.shape, jnp.float32)
    moved_by = [[(here[k] + step) % counts[k] for step in range(counts[k])] for k in range(3)]
    all_targets = [
        {"gx": moved_by[0][a], "gy": moved_by[1][b], "gz": moved_by[2][c]}
        for c in reversed(range(counts[2]))
        for b in reversed(range(counts[1]))
        for a in reversed(range(counts[0]))
        if a or b or c
    ]

    barrier = pltpu.get_barrier_semaphore()

    for target in plane_targets + line_targets:
        pl.semaphore_signal(barrier, inc=1, device_id=target, device_id_type=MESH)

    for load in loads:
        load.wait()

    table[0:1, 0 : table_in.shape[1]] = table_row[...]
    lookup = jnp.broadcast_to(table[0:1, :], (ny, LANES))
    lane = lax.broadcasted_iota(jnp.int32, (ny, LANES), 1)
    top = jnp.zeros((ny, LANES), jnp.float32)
    total = jnp.zeros((ny, LANES), jnp.float32)
    most = jnp.zeros((ny, LANES), jnp.float32)
    least = jnp.ones((ny, LANES), jnp.float32)
    for i in range(nx):
        cond = jnp.take_along_axis(lookup, ints[0, i], axis=1)
        flag = ints[1, i].astype(jnp.float32)
        grid[COND, depth + i, 0:ny, 0:nz] = cond
        grid[FLAGS, depth + i, 0:ny, 0:nz] = flag
        pieces = [
            grid[WARM, depth + i, 0:ny, 0:nz],
            cond,
            grid[SOURCE, depth + i, 0:ny, 0:nz],
            flag,
        ]
        packed = None
        for f, piece in enumerate(pieces):
            turned = pltpu.roll(piece, (f * SLOT + SLOT // 2) % LANES, 1)
            packed = turned if packed is None else jnp.where(lane // SLOT == f, turned, packed)
        edges[i] = packed
        upper = lax.broadcasted_iota(jnp.int32, (SUB, nz), 0) < SUB // 2
        last, first = slice(ny - SUB, ny), slice(0, SUB)
        mixed[0, i] = jnp.where(
            upper, pltpu.roll(flag[last], SUB // 2, 0), grid[SOURCE, depth + i, last, 0:nz]
        )
        mixed[1, i] = jnp.where(
            upper, grid[SOURCE, depth + i, first, 0:nz], pltpu.roll(flag[first], SUB // 2, 0)
        )
        top = jnp.maximum(top, cond)
        total = total + cond
        most = jnp.maximum(most, flag)
        least = jnp.minimum(least, flag)
    shrink = lambda op, v: op(op(v, axis=0, keepdims=True), axis=1, keepdims=True)
    mean = shrink(jnp.sum, total) * (1.0 / (nx * ny * nz))
    high = 1.0 + interval_delta * cooling * shrink(jnp.max, most)
    high = high + 8.0 * interval_delta * (shrink(jnp.max, top) + mean)
    low = 1.0 + interval_delta * cooling * shrink(jnp.min, least)
    row_lane = lax.broadcasted_iota(jnp.int32, (1, LANES), 1)
    row = jnp.where(row_lane == 0, high, -low)
    row_out[0] = row
    plane_rows[0, in_plane] = row

    pl.semaphore_wait(barrier, plane + line - 2)

    def remote(src, dst, send, recv, offset):
        return pltpu.make_async_remote_copy(
            src_ref=src,
            dst_ref=dst,
            send_sem=send,
            recv_sem=recv,
            device_id={a: here[k] + offset[k] for k, a in enumerate(AXES)},
            device_id_type=MESH,
        )

    def exists(offset):
        good = None
        for k in range(3):
            if offset[k] > 0:
                one = here[k] < counts[k] - 1
            elif offset[k] < 0:
                one = here[k] > 0
            else:
                continue
            good = one if good is None else jnp.logical_and(good, one)
        return good

    def share(stage, rows_ref, slot, targets):
        for target in targets:
            pltpu.make_async_remote_copy(
                src_ref=row_out.at[stage],
                dst_ref=rows_ref.at[slot],
                send_sem=row_send.at[stage],
                recv_sem=row_recv.at[stage],
                device_id=target,
                device_id_type=MESH,
            ).start()

    def share_wait(stage, rows_ref, targets):
        if targets:
            whole = pltpu.make_async_remote_copy(
                src_ref=rows_ref.at[pl.ds(0, len(targets))],
                dst_ref=rows_ref.at[pl.ds(0, len(targets))],
                send_sem=row_send.at[stage],
                recv_sem=row_recv.at[stage],
                device_id=targets[0],
                device_id_type=MESH,
            )
            whole.wait_send()
            whole.wait_recv()

    share(0, plane_rows.at[0], in_plane, plane_targets)

    z_copies = []
    for k, dz in enumerate((1, -1)):
        copy = remote(edges, beside.at[k], z_send.at[k], z_recv.at[k], (0, 0, dz))
        z_copies.append((copy, dz))
        pl.when(exists((0, 0, dz)))(copy.start)

    def ranges(offset):
        dx, dy = offset
        if dx == 0:
            xs, xd, xn = depth, depth, nx
        elif dx > 0:
            xs, xd, xn = nx, 0, depth
        else:
            xs, xd, xn = depth, depth + nx, depth
        if dy == 0:
            ys, yd, yn = 0, 0, ny
        elif dy > 0:
            ys, yd, yn = ny - SUB, ny + SUB, SUB
        else:
            ys, yd, yn = 0, ny, SUB
        z = pl.ds(0, nz)
        return (pl.ds(xs, xn), pl.ds(ys, yn), z), (pl.ds(xd, xn), pl.ds(yd, yn), z)

    offsets = [(0, 1), (0, -1), (1, 1), (-1, -1), (1, -1), (-1, 1), (1, 0), (-1, 0)]

    raw, fwd = [], []
    for k, offset in enumerate(offsets):
        src, dst = ranges(offset)
        full = offset + (0,)
        count = FIELDS if offset[1] == 0 else SOURCE
        fields = (pl.ds(0, count),)
        raw.append(
            (
                remote(
                    grid.at[fields + src], grid.at[fields + dst], raw_send.at[k], raw_recv.at[k], full
                ),
                offset,
            )
        )
        if offset[1] != 0:
            xs = pl.ds(src[0].start - depth, src[0].size)
            raw.append(
                (
                    remote(
                        mixed.at[0 if offset[1] > 0 else 1, xs],
                        grid.at[(SOURCE,) + dst],
                        mix_send.at[k],
                        mix_recv.at[k],
                        full,
                    ),
                    offset,
                )
            )
        fwd.append(
            (
                remote(
                    grid.at[(EDGES,) + src], grid.at[(EDGES,) + dst], fwd_send.at[k], fwd_recv.at[k], full
                ),
                offset,
            )
        )
    for copy, (dx, dy) in raw:
        pl.when(exists((dx, dy, 0)))(copy.start)

    for copy, dz in z_copies:
        pl.when(exists((0, 0, -dz)))(copy.wait_recv)
    low_half = lane % SLOT < SLOT // 2
    for i in range(nx):
        grid[EDGES, depth + i, 0:ny, 0:nz] = jnp.where(low_half, beside[0, i], beside[1, i])
    for copy, (dx, dy) in fwd:
        pl.when(exists((dx, dy, 0)))(copy.start)

    share_wait(0, plane_rows.at[0], plane_targets)
    row = jnp.max(plane_rows[0], axis=0)
    row_out[1] = row
    line_rows[0, here[2]] = row
    share(1, line_rows.at[0], here[2], line_targets)

    for copy, (dx, dy) in raw:
        pl.when(exists((-dx, -dy, 0)))(copy.wait_recv)
    for copy, (dx, dy) in fwd:
        pl.when(exists((-dx, -dy, 0)))(copy.wait_recv)

    batch = next(u for u in (6, 4, 2) if wide % u == 0)

    @pl.loop(0, wide // batch)
    def _(group):
        for u in range(batch):
            i = batch * group + u
            packed = grid[EDGES, i, :, 0:nz]
            grid[FLAGS, i, ny:, 0:nz] = jnp.concatenate(
                [
                    pltpu.roll(grid[SOURCE, i, ny : ny + SUB, 0:nz], SUB // 2, 0),
                    pltpu.roll(grid[SOURCE, i, ny + SUB :, 0:nz], SUB // 2, 0),
                ],
                axis=0,
            )
            for f in range(FIELDS):
                grid[f, i, :, nz:] = pltpu.roll(packed, (-f * SLOT - SLOT // 2) % LANES, 1)
            warm_flux[i] = grid[COND, i] * grid[WARM, i]

    share_wait(1, line_rows.at[0], line_targets)
    bounds = jnp.max(line_rows[0], axis=0)
    pick = lambda v, i: jnp.sum(jnp.where(row_lane == i, v, 0.0), axis=1, keepdims=True)
    high, low = pick(bounds, 0), -pick(bounds, 1)
    middle = 0.5 * (high + low)
    half = 0.5 * (high - low)
    twice = 2.0 / half

    def valid(index, size, cut, k):
        inner = index < size
        right = jnp.logical_and(index < size + cut, here[k] < counts[k] - 1)
        left = jnp.logical_and(index >= size + cut, here[k] > 0)
        return jnp.logical_or(inner, jnp.logical_or(right, left))

    def inside_of(rows, cut):
        y_index = lax.broadcasted_iota(jnp.int32, (rows, long), 0)
        z_index = lax.broadcasted_iota(jnp.int32, (rows, long), 1)
        both = jnp.logical_and(valid(y_index, ny, cut, 1), valid(z_index, nz, LANES // 2, 2))
        return jnp.where(both, 1.0, 0.0)

    x_left = jnp.where(here[0] > 0, 1.0, 0.0)
    x_right = jnp.where(here[0] < counts[0] - 1, 1.0, 0.0)

    def x_inside(i):
        return jnp.where(i < depth, x_left, jnp.where(i >= depth + nx, x_right, 1.0))

    quarter = 0.125 * interval_delta
    inside = quarter * inside_of(tall, SUB)
    first_half = lax.broadcasted_iota(jnp.int32, (SUB, long), 0) < SUB // 2

    def narrow(v):
        ends = jnp.where(first_half, v[ny : ny + SUB], v[ny + SUB :])
        return jnp.concatenate([v[:ny], ends], axis=0)

    several = next(u for u in (4, 2) if (wide - 2) % u == 0)

    @pl.loop(0, (wide - 2) // several)
    def _(group):
        for u in range(several):
            i = 1 + several * group + u
            cond = grid[COND, i]
            ring = smooth_all(grid[COND, i - 1], cond, grid[COND, i + 1])
            d = 1.0 + interval_delta * cooling * grid[FLAGS, i]
            d = d + 8.0 * interval_delta * cond + quarter * ring
            warm = grid[WARM, i]
            own = smooth_all(grid[WARM, i - 1], warm, grid[WARM, i + 1])
            push = smooth_all(warm_flux[i - 1], warm_flux[i], warm_flux[i + 1])
            image = d * warm - (quarter * cond * own + x_inside(i) * inside * push)
            left = narrow(warm + interval_delta * grid[SOURCE, i] - image)
            edge = (quarter * twice) * narrow(cond)
            basis[0, i] = left
            diag[i] = twice * (narrow(d) - middle)
            couple[i] = edge
            flux[0, i] = edge * left

    within = inside_of(short, SUB // 2)
    for k in range(ITERS):

        half_planes = wide // 2 - 2 - k

        @pl.loop(0, 2)
        def _(group):
            for u in range(half_planes):
                i = 2 + k + half_planes * group + u
                edge = couple[i]
                mid = basis[k, i]
                own = smooth_all(basis[k, i - 1], mid, basis[k, i + 1])
                push = smooth_all(flux[k % 2, i - 1], flux[k % 2, i], flux[k % 2, i + 1])
                fresh = diag[i] * mid - (edge * own + x_inside(i) * within * push)
                if k > 0:
                    fresh = fresh - basis[k - 1, i]
                basis[k + 1, i] = fresh
                if k + 1 < ITERS:
                    flux[(k + 1) % 2, i] = edge * fresh

    sums = [None] * len(PAIRS)
    for i in range(depth, depth + nx):
        rows = [basis[k, i, 0:ny, 0:nz] for k in range(ITERS + 1)]
        for n, (a, b) in enumerate(PAIRS):
            term = rows[a] * rows[b]
            sums[n] = term if sums[n] is None else sums[n] + term
    diagonal = lax.broadcasted_iota(jnp.int32, (SUB, LANES), 0)
    across = lax.broadcasted_iota(jnp.int32, (SUB, LANES), 1)
    row = jnp.zeros((SUB, LANES), jnp.float32)
    for start in range(0, len(PAIRS), SUB):
        tile = jnp.zeros((SUB, LANES), jnp.float32)
        for n in range(start, min(start + SUB, len(PAIRS))):
            tile = jnp.where(diagonal == n - start, jnp.sum(sums[n], axis=0, keepdims=True), tile)
        column = jnp.sum(tile, axis=1, keepdims=True)
        row = row + jnp.where(across == diagonal + start, column, 0.0)
    row = jnp.sum(row, axis=0, keepdims=True)
    row_out[2] = row
    if plane * line <= DIRECT:
        mine = in_plane * line + here[2]
        all_rows[mine] = row
        share(2, all_rows, mine, all_targets)
        share_wait(2, all_rows, all_targets)
        row = jnp.sum(all_rows[...], axis=0)
    else:
        plane_rows[1, in_plane] = row
        share(2, plane_rows.at[1], in_plane, plane_targets)
        share_wait(2, plane_rows.at[1], plane_targets)
        row = jnp.sum(plane_rows[1], axis=0)
        row_out[3] = row
        line_rows[1, here[2]] = row
        share(3, line_rows.at[1], here[2], line_targets)
        share_wait(3, line_rows.at[1], line_targets)
        row = jnp.sum(line_rows[1], axis=0)
    gram = {}
    for n, (a, b) in enumerate(PAIRS):
        gram[a, b] = gram[b, a] = pick(row, n)

    def apply(p):
        q = [middle * a for a in p] + [jnp.zeros_like(half)]
        for i, a in enumerate(p):
            q[i + 1] = q[i + 1] + (0.5 * half) * a
            if i > 0:
                q[i - 1] = q[i - 1] + (0.5 * half) * a
        return q

    def product(p, q):
        value = None
        for i, a in enumerate(p):
            inner = None
            for j, b in enumerate(q):
                term = gram[i, j] * b
                inner = term if inner is None else inner + term
            inner = a * inner
            value = inner if value is None else value + inner
        return value

    left = [jnp.ones_like(half)]
    heading = list(left)
    moved = []
    norm = product(left, left)
    for step in range(ITERS):
        image = apply(heading)
        alpha = norm / product(heading, image)
        moved = [a + alpha * b for a, b in zip(moved, heading)] + [
            alpha * b for b in heading[len(moved) :]
        ]
        left = [a - alpha * b for a, b in zip(left, image)] + [
            -alpha * b for b in image[len(left) :]
        ]
        if step + 1 < ITERS:
            following = product(left, left)
            ratio = following / norm
            heading = [a + ratio * b for a, b in zip(left, heading)] + left[len(heading) :]
            norm = following

    for i in range(nx):
        warm = grid[WARM, depth + i, 0:ny, 0:nz]
        end = jnp.zeros_like(warm)
        for k in range(ITERS + 1):
            value = basis[k, depth + i, 0:ny, 0:nz]
            if k < ITERS:
                warm = warm + moved[k] * value
            end = end + left[k] * value
        both_out[0, i] = warm
        both_out[1, i] = end

    for copy, dz in z_copies:
        pl.when(exists((0, 0, dz)))(copy.wait_send)
    for copy, (dx, dy) in raw + fwd:
        pl.when(exists((dx, dy, 0)))(copy.wait_send)


def body(counts, warm, source, category, table, flags):
    nx, ny, nz = warm.shape
    depth = ITERS + 1
    plane, line = counts[0] * counts[1], counts[2]
    if nx < depth or nx % 2 or ny % SUB or nz != LANES or table.shape[0] > LANES:
        raise ValueError("block shape")
    wide, tall, short, long = nx + 2 * depth, ny + 2 * SUB, ny + SUB, nz + LANES
    table = table[None]
    any_spec = pl.BlockSpec(memory_space=pl.ANY)
    vmem = pl.BlockSpec(memory_space=pltpu.VMEM)
    f32 = jnp.float32
    both = pl.pallas_call(
        functools.partial(kernel, counts),
        out_shape=pltpu.VMEM((2,) + warm.shape, jnp.float32),
        in_specs=[any_spec] * 5,
        out_specs=vmem,
        scratch_shapes=[
            pltpu.VMEM((FIELDS + 1, wide, tall, long), f32),
            pltpu.VMEM((ITERS + 1, wide, short, long), f32),
            pltpu.VMEM((2, wide, short, long), f32),
            pltpu.VMEM((wide, tall, long), f32),
            pltpu.VMEM((wide, short, long), f32),
            pltpu.VMEM((wide, short, long), f32),
            pltpu.VMEM((SUB, LANES), f32),
            pltpu.VMEM(table.shape, f32),
            pltpu.VMEM((2, nx, ny, nz), jnp.int32),
            pltpu.VMEM((nx, ny, nz), f32),
            pltpu.VMEM((2, nx, SUB, nz), f32),
            pltpu.VMEM((2, nx, ny, nz), f32),
            pltpu.VMEM((4, 1, LANES), f32),
            pltpu.VMEM((2, plane, 1, LANES), f32),
            pltpu.VMEM((2, line, 1, LANES), f32),
            pltpu.VMEM((plane * line, 1, LANES), f32),
            pltpu.SemaphoreType.DMA((5,)),
            pltpu.SemaphoreType.DMA((8,)),
            pltpu.SemaphoreType.DMA((8,)),
            pltpu.SemaphoreType.DMA((8,)),
            pltpu.SemaphoreType.DMA((8,)),
            pltpu.SemaphoreType.DMA((8,)),
            pltpu.SemaphoreType.DMA((8,)),
            pltpu.SemaphoreType.DMA((2,)),
            pltpu.SemaphoreType.DMA((2,)),
            pltpu.SemaphoreType.DMA((4,)),
            pltpu.SemaphoreType.DMA((4,)),
        ],
        compiler_params=pltpu.CompilerParams(collective_id=0, has_side_effects=True),
    )(warm, source, category, table, flags)
    return both[0], both[1]


def solution(mesh):
    counts = tuple(mesh.shape[a] for a in AXES)
    spec = P("gx", "gy", "gz")
    return jax.shard_map(
        functools.partial(body, counts),
        mesh=mesh,
        in_specs=(spec, spec, spec, P(), spec),
        out_specs=(spec, spec),
        check_vma=False,
    )
```

profile of v0, /device:TPU:0, one launch (start us, length us, event | category | flops | bytes accessed | tf_op | source)
XLA Modules:
  0.0 23.1 jit_solution(17303898409079500478)
XLA Ops:
  0.6 21.8 %shard_map.68 = f32[2,8,16,128]{3,2,1,0:T(8,128)S(1)} custom-call(f32[8,16,128]{2,1,0:T(8,128)} %warm_in.1, f32[8,16,128]{2,1,0:T(8,128)} %source_in.1, s32[8,16,128]{2,1,0:T(8,128)} %category_in.1, f32[1,16]{1,0:T(1,128)} %bitcast.5, s32[8,16,128]{2,1,0:T(8,128)} %flags_in.1), custom_call_target="tpu_custom_call" | custom-call | tf_op jit(solution)/shard_map/pallas_call | solution.py:496
  22.4 0.7 %slice_bitcast_fusion = (f32[8,16,128]{2,1,0:T(8,128)}, f32[8,16,128]{2,1,0:T(8,128)}) fusion(f32[2,8,16,128]{3,2,1,0:T(8,128)S(1)} %shard_map.68), kind=kLoop, calls=%fused_computation | loop fusion | bytes 262144 | tf_op jit(solution)/shard_map/squeeze | solution.py:532
where the time goes:
time: 23.3 us; the launch traced here: 23.1 us
  Pallas kernels  21.8 us (94%)
  local copies, waits for them, and re-layouts  0.66 us (3%)
  between operations  0.64 us (3%)
    pallas_call x1, Pallas kernels, body(): pl.pallas_call(functools.partial(kernel, counts), out_shape=pltpu.VMEM((2...  21.8 us
    squeeze x1, local copies, waits for them, and re-layouts, body(): return (both[0], both[1])  0.66 us

commit v1 on v0

v1 whole, which is shorter than its diff:
```python
import functools

import jax
import jax.numpy as jnp
from jax import lax
from jax.experimental import pallas as pl
from jax.experimental.pallas import tpu as pltpu
from jax.sharding import PartitionSpec as P

ITERS = 4
interval_delta = 2.0
cooling = 3.0

MESH = pl.DeviceIdType.MESH
AXES = ("gx", "gy", "gz")
SUB = 8
REACH = 4
LANES = 128
FIELDS = 4
DEPTH = ITERS + 1
SLOT = 2 * DEPTH
PER = LANES // (FIELDS * SLOT)
PAIRS = [(i, j) for i in range(ITERS + 1) for j in range(i, ITERS + 1) if i < ITERS]
WAYS = [(a, b, c) for a in (0, 1, -1) for b in (0, 1, -1) for c in (0, 1, -1) if a or b or c]


def smooth(values, axis):
    size = values.shape[axis]
    return (values + values) + (pltpu.roll(values, 1, axis) + pltpu.roll(values, size - 1, axis))


def smooth_all(before, center, after):
    return smooth(smooth(before + (center + center) + after, 0), 1)


def kernel(
    counts,
    warm_in,
    source_in,
    category_in,
    table_in,
    flags_in,
    both_out,
    pair,
    push_in,
    cool,
    basis,
    flux,
    warm_flux,
    diag,
    couple,
    table,
    table_row,
    source,
    ints,
    edges,
    beside,
    row_out,
    plane_rows,
    line_rows,
    all_rows,
    load_sems,
    halo_send,
    halo_recv,
    row_send,
    row_recv,
    near,
    far,
):
    plane, line = counts[0] * counts[1], counts[2]
    nx, ny, nz = both_out.shape[1:]
    depth = DEPTH
    wide, tall, long = pair.shape[1:]
    short = ny + SUB
    groups = edges.shape[0]
    ends = -(-depth // PER)
    last = (nx - depth) // PER
    direct = max(counts) <= REACH
    here = [lax.axis_index(a) for a in AXES]
    in_plane = here[0] * counts[1] + here[1]

    def exists(offset):
        good = None
        for k in range(3):
            if offset[k] > 0:
                one = here[k] < counts[k] - offset[k]
            elif offset[k] < 0:
                one = here[k] >= -offset[k]
            else:
                continue
            good = one if good is None else jnp.logical_and(good, one)
        return good

    def at(offset):
        return {a: here[k] + offset[k] for k, a in enumerate(AXES)}

    def back(offset):
        return tuple(-o for o in offset)

    def signal(semaphore, offset):
        @pl.when(exists(offset))
        def _():
            pl.semaphore_signal(semaphore, inc=1, device_id=at(offset), device_id_type=MESH)

    def present(offsets):
        return sum(jnp.where(exists(offset), 1, 0) for offset in offsets)

    plane_targets = [
        {"gx": other // counts[1], "gy": other % counts[1], "gz": here[2]}
        for other in [(in_plane + step) % plane for step in range(1, plane)]
    ]
    line_targets = [
        {"gx": here[0], "gy": here[1], "gz": (here[2] + step) % line} for step in range(1, line)
    ]
    moved_by = [[(here[k] + step) % counts[k] for step in range(counts[k])] for k in range(3)]
    all_targets = [
        {"gx": moved_by[0][a], "gy": moved_by[1][b], "gz": moved_by[2][c]}
        for c in reversed(range(counts[2]))
        for b in reversed(range(counts[1]))
        for a in reversed(range(counts[0]))
        if a or b or c
    ]

    barrier = pltpu.get_barrier_semaphore()
    ways = [w for w in WAYS if all(abs(w[k]) < counts[k] for k in range(3))]
    for way in reversed(ways):
        signal(barrier, way)
    if not direct:
        for target in plane_targets + line_targets:
            pl.semaphore_signal(barrier, inc=1, device_id=target, device_id_type=MESH)

    own = (pl.ds(depth, nx), pl.ds(0, ny), pl.ds(0, nz))
    loads = [
        pltpu.make_async_copy(table_in, table_row, load_sems.at[4]),
        pltpu.make_async_copy(category_in, ints.at[0], load_sems.at[0]),
        pltpu.make_async_copy(flags_in, ints.at[1], load_sems.at[1]),
        pltpu.make_async_copy(warm_in, pair.at[(0,) + own], load_sems.at[2]),
        pltpu.make_async_copy(source_in, source, load_sems.at[3]),
    ]
    for load in loads:
        load.start()

    def clear(ref, *index):
        shape = ref.at[index].shape
        ref[index] = jnp.zeros(shape, jnp.float32)

    table[...] = jnp.zeros(table.shape, jnp.float32)
    body = slice(0, nz)
    for way, planes, slots in (
        ((-1, 0, 0), slice(0, depth), slice(0, ends)),
        ((1, 0, 0), slice(depth + nx, wide), slice(ends + groups, None)),
    ):

        @pl.when(jnp.logical_not(exists(way)))
        def _():
            for f in range(2):
                clear(pair, f, planes, slice(None), body)
            clear(push_in, planes, slice(None), body)
            clear(cool, planes, slice(None), body)
            for side in range(2):
                clear(beside, side, slots, slice(None), slice(None))

    for way, rows, few in (
        ((0, 1, 0), slice(ny, ny + SUB), slice(ny, ny + SUB // 2)),
        ((0, -1, 0), slice(tall - SUB, tall), slice(short - SUB // 2, short)),
    ):

        @pl.when(jnp.logical_not(exists(way)))
        def _():
            for f in range(2):
                clear(pair, f, slice(None), rows, body)
            clear(push_in, slice(None), few, body)
            clear(cool, slice(None), few, body)
            for side in range(2):
                clear(beside, side, slice(None), rows, slice(None))

    for side, way in enumerate(((0, 0, -1), (0, 0, 1))):

        @pl.when(jnp.logical_not(exists(way)))
        def _():
            clear(beside, side, slice(None), slice(None), slice(None))

    for load in loads:
        load.wait()

    table[0:1, 0 : table_in.shape[1]] = table_row[...]
    lookup = jnp.broadcast_to(table[0:1, :], (ny, LANES))
    lane = lax.broadcasted_iota(jnp.int32, (ny, LANES), 1)
    for start in range(0, nx, PER):
        packed = None
        for i in range(start, min(start + PER, nx)):
            cond = jnp.take_along_axis(lookup, ints[0, i], axis=1)
            flag = ints[1, i].astype(jnp.float32)
            warm = pair[0, depth + i, 0:ny, 0:nz]
            push = interval_delta * source[i] - (interval_delta * cooling) * flag * warm
            pair[1, depth + i, 0:ny, 0:nz] = cond
            cool[depth + i, 0:ny, 0:nz] = flag
            push_in[depth + i, 0:ny, 0:nz] = push
            for f, piece in enumerate((warm, cond, push, flag)):
                q = (i - start) * FIELDS + f
                turned = pltpu.roll(piece, (q * SLOT + depth) % LANES, 1)
                packed = turned if packed is None else jnp.where(lane >= q * SLOT, turned, packed)
        edges[start // PER] = packed

    most = 7.0 + 24.0 * jnp.max(table[0:1, :], axis=1, keepdims=True)
    high, low = most, jnp.ones_like(most)
    middle = 0.5 * (high + low)
    half = 0.5 * (high - low)
    twice = 2.0 / half

    waits = present(back(w) for w in ways)
    if not direct:
        waits = waits + (plane + line - 2)
    pl.semaphore_wait(barrier, waits)

    def span(step, size, total, least, most):
        if step == 0:
            return pl.ds(least, size), pl.ds(least, size)
        if step > 0:
            return pl.ds(least + size - total, total), pl.ds(most - total, total)
        return pl.ds(least, total), pl.ds(least + size, total)

    def xspan(step, size, total):
        if step == 0:
            return pl.ds(depth, size), pl.ds(depth, size)
        if step > 0:
            return pl.ds(depth + size - total, total), pl.ds(depth - total, total)
        return pl.ds(depth, total), pl.ds(depth + size, total)

    halos = []

    def send(src, dst, way):
        k = len(halos)
        copy = pltpu.make_async_remote_copy(
            src_ref=src,
            dst_ref=dst,
            send_sem=halo_send.at[k],
            recv_sem=halo_recv.at[k],
            device_id=at(way),
            device_id_type=MESH,
        )
        pl.when(exists(way))(copy.start)
        halos.append((copy, way))

    def send_edges(way):
        dx, dy, dz = way
        if dx == 0:
            src_x, dst_x = pl.ds(0, groups), pl.ds(ends, groups)
        elif dx > 0:
            src_x, dst_x = pl.ds(last, groups - last), pl.ds(0, groups - last)
        else:
            src_x, dst_x = pl.ds(0, ends), pl.ds(ends + groups, ends)
        src_y, dst_y = span(dy, ny, depth, 0, tall)
        send(edges.at[src_x, src_y], beside.at[0 if dz > 0 else 1, dst_x, dst_y], way)

    def send_fields(way):
        dx, dy = way[:2]
        z = pl.ds(0, nz)
        src_x, dst_x = xspan(dx, nx, depth)
        src_y, dst_y = span(dy, ny, depth, 0, tall)
        both = pl.ds(0, 2)
        send(pair.at[both, src_x, src_y, z], pair.at[both, dst_x, dst_y, z], way)
        for ref, less in ((push_in, 1), (cool, 2)):
            src_x, dst_x = xspan(dx, nx, depth - less)
            src_y, dst_y = span(dy, ny, depth - less, 0, short)
            send(ref.at[src_x, src_y, z], ref.at[dst_x, dst_y, z], way)

    for way in sorted(ways, key=lambda w: -sum(map(abs, w))):
        if way[2]:
            send_edges(way)
    for way in sorted(ways, key=lambda w: -sum(map(abs, w))):
        if not way[2]:
            send_fields(way)
    if direct:
        for way in ways:
            signal(near, way)
        hops = [(a, 0, c) for a in (0, 2, -2) for c in (0, 2, -2) if a or c]
        hops = [h for h in hops if abs(h[0]) < counts[0] and abs(h[2]) < counts[2]]
        pl.semaphore_wait(near, present(back(w) for w in ways))
        for hop in hops:
            signal(far, hop)

    def share(stage, rows_ref, slot, targets):
        for target in targets:
            pltpu.make_async_remote_copy(
                src_ref=row_out.at[stage],
                dst_ref=rows_ref.at[slot],
                send_sem=row_send.at[stage],
                recv_sem=row_recv.at[stage],
                device_id=target,
                device_id_type=MESH,
            ).start()

    def share_wait(stage, rows_ref, targets):
        if targets:
            whole = pltpu.make_async_remote_copy(
                src_ref=rows_ref.at[pl.ds(0, len(targets))],
                dst_ref=rows_ref.at[pl.ds(0, len(targets))],
                send_sem=row_send.at[stage],
                recv_sem=row_recv.at[stage],
                device_id=targets[0],
                device_id_type=MESH,
            )
            whole.wait_send()
            whole.wait_recv()

    for copy, way in halos:
        pl.when(exists(back(way)))(copy.wait_recv)

    first_half = lax.broadcasted_iota(jnp.int32, (SUB, LANES), 0) < SUB // 2
    all_lanes = lax.broadcasted_iota(jnp.int32, (tall, LANES), 1)
    left_side = all_lanes % SLOT < depth

    def narrow(v):
        mask = jnp.concatenate([first_half] * (v.shape[1] // LANES), axis=1)
        join = jnp.where(mask, v[ny : ny + SUB], v[ny + SUB :])
        return jnp.concatenate([v[:ny], join], axis=0)

    regions = [(0, ends, 0, depth, nx - depth - last * PER)]
    regions += [(ends, groups, depth, nx, 0), (ends + groups, ends, depth + nx, depth, 0)]
    for first_group, some, first_plane, planes, skip in regions:
        for g in range(some):
            merged = jnp.where(left_side, beside[0, first_group + g], beside[1, first_group + g])
            thin = narrow(merged)
            for s in range(PER):
                j = g * PER + s - skip
                if not 0 <= j < planes:
                    continue
                i = first_plane + j
                shifts = [-((s * FIELDS + f) * SLOT + depth) % LANES for f in range(FIELDS)]
                for f in range(2):
                    pair[f, i, :, nz:] = pltpu.roll(merged, shifts[f], 1)
                if 1 <= i < wide - 1:
                    push_in[i, :, nz:] = pltpu.roll(thin, shifts[2], 1)
                if 2 <= i < wide - 2:
                    cool[i, :, nz:] = pltpu.roll(thin, shifts[3], 1)
                warm_flux[i] = pair[0, i] * pair[1, i]

    def valid(index, size, cut, k):
        inner = index < size
        right = jnp.logical_and(index < size + cut, here[k] < counts[k] - 1)
        left = jnp.logical_and(index >= size + cut, here[k] > 0)
        return jnp.logical_or(inner, jnp.logical_or(right, left))

    def inside_of(rows, cut):
        y_index = lax.broadcasted_iota(jnp.int32, (rows, long), 0)
        z_index = lax.broadcasted_iota(jnp.int32, (rows, long), 1)
        both = jnp.logical_and(valid(y_index, ny, cut, 1), valid(z_index, nz, LANES // 2, 2))
        return jnp.where(both, 1.0, 0.0)

    x_left = jnp.where(here[0] > 0, 1.0, 0.0)
    x_right = jnp.where(here[0] < counts[0] - 1, 1.0, 0.0)

    def x_inside(i):
        return jnp.where(i < depth, x_left, jnp.where(i >= depth + nx, x_right, 1.0))

    quarter = 0.125 * interval_delta
    within = inside_of(short, SUB // 2)
    inside = quarter * within
    several = next(u for u in (4, 2) if (wide - 2) % u == 0)

    @pl.loop(0, (wide - 2) // several)
    def _(group):
        for u in range(several):
            i = 1 + several * group + u
            cond = narrow(pair[1, i])
            warm = narrow(pair[0, i])
            ring = narrow(smooth_all(pair[1, i - 1], pair[1, i], pair[1, i + 1]))
            near_warm = narrow(smooth_all(pair[0, i - 1], pair[0, i], pair[0, i + 1]))
            push = narrow(smooth_all(warm_flux[i - 1], warm_flux[i], warm_flux[i + 1]))
            spread = 8.0 * interval_delta * cond + quarter * ring
            image = spread * warm - (quarter * cond * near_warm + x_inside(i) * inside * push)
            left = push_in[i] - image
            edge = (quarter * twice) * cond
            basis[0, i] = left
            diag[i] = twice * (spread + (1.0 - middle) + interval_delta * cooling * cool[i])
            couple[i] = edge
            flux[0, i] = edge * left
    for k in range(ITERS):

        half_planes = wide // 2 - 2 - k

        @pl.loop(0, 2)
        def _(group):
            for u in range(half_planes):
                i = 2 + k + half_planes * group + u
                edge = couple[i]
                mid = basis[k, i]
                own = smooth_all(basis[k, i - 1], mid, basis[k, i + 1])
                push = smooth_all(flux[k % 2, i - 1], flux[k % 2, i], flux[k % 2, i + 1])
                fresh = diag[i] * mid - (edge * own + x_inside(i) * within * push)
                if k > 0:
                    fresh = fresh - basis[k - 1, i]
                basis[k + 1, i] = fresh
                if k + 1 < ITERS:
                    flux[(k + 1) % 2, i] = edge * fresh

    sums = [None] * len(PAIRS)
    for i in range(depth, depth + nx):
        rows = [basis[k, i, 0:ny, 0:nz] for k in range(ITERS + 1)]
        for n, (a, b) in enumerate(PAIRS):
            term = rows[a] * rows[b]
            sums[n] = term if sums[n] is None else sums[n] + term
    diagonal = lax.broadcasted_iota(jnp.int32, (SUB, LANES), 0)
    across = lax.broadcasted_iota(jnp.int32, (SUB, LANES), 1)
    row = jnp.zeros((SUB, LANES), jnp.float32)
    for start in range(0, len(PAIRS), SUB):
        tile = jnp.zeros((SUB, LANES), jnp.float32)
        for n in range(start, min(start + SUB, len(PAIRS))):
            tile = jnp.where(diagonal == n - start, jnp.sum(sums[n], axis=0, keepdims=True), tile)
        column = jnp.sum(tile, axis=1, keepdims=True)
        row = row + jnp.where(across == diagonal + start, column, 0.0)
    row = jnp.sum(row, axis=0, keepdims=True)
    row_out[0] = row
    if direct:
        pl.semaphore_wait(far, present(back(h) for h in hops))
        mine = in_plane * line + here[2]
        all_rows[mine] = row
        share(0, all_rows, mine, all_targets)
        share_wait(0, all_rows, all_targets)
        row = jnp.sum(all_rows[...], axis=0)
    else:
        plane_rows[in_plane] = row
        share(0, plane_rows, in_plane, plane_targets)
        share_wait(0, plane_rows, plane_targets)
        row = jnp.sum(plane_rows[...], axis=0)
        row_out[1] = row
        line_rows[here[2]] = row
        share(1, line_rows, here[2], line_targets)
        share_wait(1, line_rows, line_targets)
        row = jnp.sum(line_rows[...], axis=0)
    row_lane = lax.broadcasted_iota(jnp.int32, (1, LANES), 1)
    pick = lambda v, i: jnp.sum(jnp.where(row_lane == i, v, 0.0), axis=1, keepdims=True)
    gram = {}
    for n, (a, b) in enumerate(PAIRS):
        gram[a, b] = gram[b, a] = pick(row, n)

    def apply(p):
        q = [middle * a for a in p] + [jnp.zeros_like(half)]
        for i, a in enumerate(p):
            q[i + 1] = q[i + 1] + (0.5 * half) * a
            if i > 0:
                q[i - 1] = q[i - 1] + (0.5 * half) * a
        return q

    def product(p, q):
        value = None
        for i, a in enumerate(p):
            inner = None
            for j, b in enumerate(q):
                term = gram[i, j] * b
                inner = term if inner is None else inner + term
            inner = a * inner
            value = inner if value is None else value + inner
        return value

    left = [jnp.ones_like(half)]
    heading = list(left)
    moved = []
    norm = product(left, left)
    for step in range(ITERS):
        image = apply(heading)
        alpha = norm / product(heading, image)
        moved = [a + alpha * b for a, b in zip(moved, heading)] + [
            alpha * b for b in heading[len(moved) :]
        ]
        left = [a - alpha * b for a, b in zip(left, image)] + [
            -alpha * b for b in image[len(left) :]
        ]
        if step + 1 < ITERS:
            following = product(left, left)
            ratio = following / norm
            heading = [a + ratio * b for a, b in zip(left, heading)] + left[len(heading) :]
            norm = following

    for i in range(nx):
        warm = pair[0, depth + i, 0:ny, 0:nz]
        end = jnp.zeros_like(warm)
        for k in range(ITERS + 1):
            value = basis[k, depth + i, 0:ny, 0:nz]
            if k < ITERS:
                warm = warm + moved[k] * value
            end = end + left[k] * value
        both_out[0, i] = warm
        both_out[1, i] = end

    for copy, way in halos:
        pl.when(exists(way))(copy.wait_send)


def body(counts, warm, source, category, table, flags):
    nx, ny, nz = warm.shape
    depth = DEPTH
    groups, ends = -(-nx // PER), -(-depth // PER)
    copies = 8 * 3 + 18
    plane, line = counts[0] * counts[1], counts[2]
    if nx < depth or nx % 2 or ny % SUB or nz != LANES or table.shape[0] > LANES:
        raise ValueError("block shape")
    if groups - (nx - depth) // PER != ends:
        raise ValueError("block shape")
    wide, tall, short, long = nx + 2 * depth, ny + 2 * SUB, ny + SUB, nz + LANES
    table = table[None]
    any_spec = pl.BlockSpec(memory_space=pl.ANY)
    vmem = pl.BlockSpec(memory_space=pltpu.VMEM)
    f32 = jnp.float32
    both = pl.pallas_call(
        functools.partial(kernel, counts),
        out_shape=pltpu.VMEM((2,) + warm.shape, jnp.float32),
        in_specs=[any_spec] * 5,
        out_specs=vmem,
        scratch_shapes=[
            pltpu.VMEM((2, wide, tall, long), f32),
            pltpu.VMEM((wide, short, long), f32),
            pltpu.VMEM((wide, short, long), f32),
            pltpu.VMEM((ITERS + 1, wide, short, long), f32),
            pltpu.VMEM((2, wide, short, long), f32),
            pltpu.VMEM((wide, tall, long), f32),
            pltpu.VMEM((wide, short, long), f32),
            pltpu.VMEM((wide, short, long), f32),
            pltpu.VMEM((SUB, LANES), f32),
            pltpu.VMEM(table.shape, f32),
            pltpu.VMEM((nx, ny, nz), f32),
            pltpu.VMEM((2, nx, ny, nz), jnp.int32),
            pltpu.VMEM((groups, ny, nz), f32),
            pltpu.VMEM((2, groups + 2 * ends, tall, nz), f32),
            pltpu.VMEM((2, 1, LANES), f32),
            pltpu.VMEM((plane, 1, LANES), f32),
            pltpu.VMEM((line, 1, LANES), f32),
            pltpu.VMEM((plane * line, 1, LANES), f32),
            pltpu.SemaphoreType.DMA((5,)),
            pltpu.SemaphoreType.DMA((copies,)),
            pltpu.SemaphoreType.DMA((copies,)),
            pltpu.SemaphoreType.DMA((2,)),
            pltpu.SemaphoreType.DMA((2,)),
            pltpu.SemaphoreType.REGULAR,
            pltpu.SemaphoreType.REGULAR,
        ],
        compiler_params=pltpu.CompilerParams(collective_id=0, has_side_effects=True),
    )(warm, source, category, table, flags)
    return both[0], both[1]


def solution(mesh):
    counts = tuple(mesh.shape[a] for a in AXES)
    spec = P("gx", "gy", "gz")
    return jax.shard_map(
        functools.partial(body, counts),
        mesh=mesh,
        in_specs=(spec, spec, spec, P(), spec),
        out_specs=(spec, spec),
        check_vma=False,
    )
```

time: 23.3 us -> 21.2 us (0.910)
  Pallas kernels: 21.8 us -> 19.7 us
    pallas_call x1, Pallas kernels: 21.8 us -> 19.7 us  [body(): pl.pallas_call(functools.partial(kernel, counts), out_shape=pltpu.VMEM((2...]
where the time goes in v1:
time: 21.2 us; the launch traced here: 21 us
  Pallas kernels  19.7 us (93%)
  local copies, waits for them, and re-layouts  0.66 us (3%)
  between operations  0.64 us (3%)
    pallas_call x1, Pallas kernels, body(): pl.pallas_call(functools.partial(kernel, counts), out_shape=pltpu.VMEM((2...  19.7 us
    squeeze x1, local copies, waits for them, and re-layouts, body(): return (both[0], both[1])  0.66 us

profile of v1, /device:TPU:0, one launch (start us, length us, event | category | flops | bytes accessed | tf_op | source)
XLA Modules:
  0.0 21.0 jit_solution(2716512572683723754)
XLA Ops:
  0.6 19.7 %shard_map.68 = f32[2,8,16,128]{3,2,1,0:T(8,128)S(1)} custom-call(f32[8,16,128]{2,1,0:T(8,128)} %warm_in.1, f32[8,16,128]{2,1,0:T(8,128)} %source_in.1, s32[8,16,128]{2,1,0:T(8,128)} %category_in.1, f32[1,16]{1,0:T(1,128)} %bitcast.5, s32[8,16,128]{2,1,0:T(8,128)} %flags_in.1), custom_call_target="tpu_custom_call" | custom-call | tf_op jit(solution)/shard_map/pallas_call | solution.py:506
  20.3 0.7 %slice_bitcast_fusion = (f32[8,16,128]{2,1,0:T(8,128)}, f32[8,16,128]{2,1,0:T(8,128)}) fusion(f32[2,8,16,128]{3,2,1,0:T(8,128)S(1)} %shard_map.68), kind=kLoop, calls=%fused_computation | loop fusion | bytes 262144 | tf_op jit(solution)/shard_map/squeeze | solution.py:540

commit v2 on v1

v2 whole, which is shorter than its diff:
```python
import functools

import jax
import jax.numpy as jnp
from jax import lax
from jax.experimental import pallas as pl
from jax.experimental.pallas import tpu as pltpu
from jax.sharding import PartitionSpec as P

ITERS = 4
interval_delta = 2.0
cooling = 3.0

MESH = pl.DeviceIdType.MESH
AXES = ("gx", "gy", "gz")
SUB = 8
REACH = 4
LANES = 128
FIELDS = 4
DEPTH = ITERS + 1
SLOT = 2 * DEPTH
PER = LANES // (FIELDS * SLOT)
MOMENTS = 2 * ITERS
REGIONS = [(a, c) for c in (0, 1, -1) for a in (0, 1, -1)]


def smooth_y(values):
    pairs = values + pltpu.roll(values, 1, 0)
    return pairs + pltpu.roll(pairs, values.shape[0] - 1, 0)


def smooth_z(values):
    size = values.shape[1]
    return (values + values) + (pltpu.roll(values, 1, 1) + pltpu.roll(values, size - 1, 1))


def smooth_z_own(values):
    size = values.shape[1] // 2
    main, side = values[:, :size], values[:, size:]
    lane = lax.broadcasted_iota(jnp.int32, main.shape, 1)
    before = pltpu.roll(jnp.where(lane == size - 1, side, main), 1, 1)
    after = pltpu.roll(jnp.where(lane == 0, side, main), size - 1, 1)
    return (main + main) + (before + after)


def kernel(
    counts,
    warm_in,
    source_in,
    category_in,
    table_in,
    flags_in,
    both_out,
    pair,
    push_in,
    cool,
    basis,
    flux,
    spread,
    diag,
    couple,
    masks,
    table,
    table_row,
    source,
    ints,
    edges,
    beside,
    ledger,
    row_out,
    plane_rows,
    line_rows,
    all_rows,
    load_sems,
    halo_send,
    halo_recv,
    row_send,
    row_recv,
    near,
    far,
):
    plane, line = counts[0] * counts[1], counts[2]
    nx, ny, nz = both_out.shape[1:]
    depth = DEPTH
    wide, tall, long = pair.shape[1:]
    short = ny + SUB
    groups = edges.shape[0]
    ends = -(-depth // PER)
    last = (nx - depth) // PER
    direct = max(counts) <= REACH
    here = [lax.axis_index(a) for a in AXES]
    in_plane = here[0] * counts[1] + here[1]

    def exists(offset):
        good = None
        for k in range(3):
            if offset[k] > 0:
                one = here[k] < counts[k] - offset[k]
            elif offset[k] < 0:
                one = here[k] >= -offset[k]
            else:
                continue
            good = one if good is None else jnp.logical_and(good, one)
        return good

    def at(offset):
        return {a: here[k] + offset[k] for k, a in enumerate(AXES)}

    def back(offset):
        return tuple(-o for o in offset)

    def signal(semaphore, offset):
        @pl.when(exists(offset))
        def _():
            pl.semaphore_signal(semaphore, inc=1, device_id=at(offset), device_id_type=MESH)

    def present(offsets):
        return sum(jnp.where(exists(offset), 1, 0) for offset in offsets)

    plane_targets = [
        {"gx": other // counts[1], "gy": other % counts[1], "gz": here[2]}
        for other in [(in_plane + step) % plane for step in range(1, plane)]
    ]
    line_targets = [
        {"gx": here[0], "gy": here[1], "gz": (here[2] + step) % line} for step in range(1, line)
    ]
    moved_by = [[(here[k] + step) % counts[k] for step in range(counts[k])] for k in range(3)]
    all_targets = [
        {"gx": moved_by[0][a], "gy": moved_by[1][b], "gz": moved_by[2][c]}
        for c in reversed(range(counts[2]))
        for b in reversed(range(counts[1]))
        for a in reversed(range(counts[0]))
        if a or b or c
    ]

    regions = [r for r in REGIONS if abs(r[0]) < counts[0] and abs(r[1]) < counts[2]]

    def by_class(act):
        if counts[1] == 1:
            act((0,))
            return
        pl.when(here[1] == 0)(lambda: act((0, 1)))
        pl.when(here[1] == counts[1] - 1)(lambda: act((0, -1)))
        if counts[1] > 2:
            inner = jnp.logical_and(here[1] > 0, here[1] < counts[1] - 1)
            pl.when(inner)(lambda: act((0, 1, -1)))

    def guard(region, act):
        if region == (0, 0):
            act()
        else:
            pl.when(exists((region[0], 0, region[1])))(act)

    def ways_of(region, steps):
        ways = [(region[0], step, region[1]) for step in sorted(steps, key=lambda v: -abs(v))]
        return [way for way in ways if any(way)]

    def neighbours():
        total = 0
        for region in regions:
            here_too = 1 if region == (0, 0) else jnp.where(exists((region[0], 0, region[1])), 1, 0)
            beside_y = present([(0, 1, 0), (0, -1, 0)]) if counts[1] > 1 else 0
            total = total + here_too * (beside_y + (0 if region == (0, 0) else 1))
        return total

    def signal_all(semaphore):
        def act(steps):
            for region in reversed(regions):

                def go(region=region):
                    for way in ways_of(region, steps):
                        pl.semaphore_signal(semaphore, inc=1, device_id=at(way), device_id_type=MESH)

                guard(region, go)

        by_class(act)

    own = (pl.ds(depth, nx), pl.ds(0, ny), pl.ds(0, nz))
    loads = [
        pltpu.make_async_copy(table_in, table_row, load_sems.at[0]),
        pltpu.make_async_copy(category_in, ints.at[0], load_sems.at[1]),
        pltpu.make_async_copy(flags_in, ints.at[1], load_sems.at[1]),
        pltpu.make_async_copy(warm_in, pair.at[(0,) + own], load_sems.at[1]),
        pltpu.make_async_copy(source_in, source, load_sems.at[1]),
    ]
    for load in loads:
        load.start()

    barrier = pltpu.get_barrier_semaphore()
    signal_all(barrier)
    if not direct:
        for target in plane_targets + line_targets:
            pl.semaphore_signal(barrier, inc=1, device_id=target, device_id_type=MESH)

    def clear(ref, *index):
        shape = ref.at[index].shape
        ref[index] = jnp.zeros(shape, jnp.float32)

    table[...] = jnp.zeros(table.shape, jnp.float32)
    body = slice(0, nz)
    for way, planes, slots in (
        ((-1, 0, 0), slice(0, depth), slice(0, ends)),
        ((1, 0, 0), slice(depth + nx, wide), slice(ends + groups, None)),
    ):

        @pl.when(jnp.logical_not(exists(way)))
        def _():
            for f in range(2):
                clear(pair, f, planes, slice(None), body)
            clear(push_in, planes, slice(None), body)
            clear(cool, planes, slice(None), body)
            for side in range(2):
                clear(beside, side, slots, slice(None), slice(None))

    for way, rows, few in (
        ((0, 1, 0), slice(ny, ny + SUB), slice(ny, ny + SUB // 2)),
        ((0, -1, 0), slice(tall - SUB, tall), slice(short - SUB // 2, short)),
    ):

        @pl.when(jnp.logical_not(exists(way)))
        def _():
            for f in range(2):
                clear(pair, f, slice(None), rows, body)
            clear(push_in, slice(None), few, body)
            clear(cool, slice(None), few, body)
            for side in range(2):
                clear(beside, side, slice(None), rows, slice(None))

    for side, way in enumerate(((0, 0, -1), (0, 0, 1))):

        @pl.when(jnp.logical_not(exists(way)))
        def _():
            clear(beside, side, slice(None), slice(None), slice(None))

    def valid(index, size, cut, k):
        inner = index < size
        right = jnp.logical_and(index < size + cut, here[k] < counts[k] - 1)
        left = jnp.logical_and(index >= size + cut, here[k] > 0)
        return jnp.logical_or(inner, jnp.logical_or(right, left))

    y_index = lax.broadcasted_iota(jnp.int32, (short, long), 0)
    z_index = lax.broadcasted_iota(jnp.int32, (short, long), 1)
    both_in = jnp.logical_and(valid(y_index, ny, SUB // 2, 1), valid(z_index, nz, LANES // 2, 2))
    within = jnp.where(both_in, 1.0, 0.0)
    masks[0] = jnp.where(here[0] > 0, 1.0, 0.0) * within
    masks[1] = within
    masks[2] = jnp.where(here[0] < counts[0] - 1, 1.0, 0.0) * within

    def inside(i):
        return masks[0 if i < depth else 2 if i >= depth + nx else 1]

    loads[0].wait()
    table[0:1, 0 : table_in.shape[1]] = table_row[...]
    most = 7.0 + 24.0 * jnp.max(table[0:1, :], axis=1, keepdims=True)
    high, low = most, jnp.ones_like(most)
    middle = 0.5 * (high + low)
    half = 0.5 * (high - low)
    twice = 2.0 / half
    quarter = 0.125 * interval_delta
    lookup = jnp.broadcast_to(table[0:1, :], (ny, LANES))
    lane = lax.broadcasted_iota(jnp.int32, (ny, LANES), 1)

    every = ledger.at[pl.ds(0, 4 * nx * ny)]
    pltpu.make_async_copy(every, every, load_sems.at[1]).wait()
    for start in range(0, nx, PER):
        packed = None
        for i in range(start, min(start + PER, nx)):
            cond = jnp.take_along_axis(lookup, ints[0, i], axis=1)
            flag = ints[1, i].astype(jnp.float32)
            warm = pair[0, depth + i, 0:ny, 0:nz]
            push = interval_delta * source[i] - (interval_delta * cooling) * flag * warm
            push = twice * push
            pair[1, depth + i, 0:ny, 0:nz] = cond
            cool[depth + i, 0:ny, 0:nz] = flag
            push_in[depth + i, 0:ny, 0:nz] = push
            for f, piece in enumerate((warm, cond, push, flag)):
                q = (i - start) * FIELDS + f
                turned = pltpu.roll(piece, (q * SLOT + depth) % LANES, 1)
                packed = turned if packed is None else jnp.where(lane >= q * SLOT, turned, packed)
        edges[start // PER] = packed

    waits = neighbours()
    if not direct:
        waits = waits + (plane + line - 2)
    pl.semaphore_wait(barrier, waits)

    def y_span(step, reach, full):
        if step == 0:
            return pl.ds(0, ny), pl.ds(0, ny)
        if step > 0:
            return pl.ds(ny - reach, reach), pl.ds(full - reach, reach)
        return pl.ds(0, reach), pl.ds(ny, reach)

    def x_span(step, reach):
        if step == 0:
            return pl.ds(depth, nx), pl.ds(depth, nx)
        if step > 0:
            return pl.ds(depth + nx - reach, reach), pl.ds(depth - reach, reach)
        return pl.ds(depth, reach), pl.ds(depth + nx, reach)

    def send(src, dst, way, stage):
        region = (way[0], way[2])
        pltpu.make_async_remote_copy(
            src_ref=src,
            dst_ref=dst,
            send_sem=halo_send.at[REGIONS.index(region)],
            recv_sem=halo_recv.at[stage + REGIONS.index((-way[0], -way[2]))],
            device_id=at(way),
            device_id_type=MESH,
        ).start()

    def send_field(view, way, reach, full, stage):
        src_x, dst_x = x_span(way[0], reach)
        src_y, dst_y = y_span(way[1], reach, full)
        z = pl.ds(0, nz)
        send(view(src_x, src_y, z), view(dst_x, dst_y, z), way, stage)

    def send_first(way):
        send_field(lambda *v: pair.at[(1,) + v], way, depth, tall, 0)
        send_field(lambda *v: cool.at[v], way, depth - 2, short, 0)

    def send_second(way):
        send_field(lambda *v: pair.at[(0,) + v], way, depth, tall, 9)
        send_field(lambda *v: push_in.at[v], way, depth - 1, short, 9)

    def send_edges(way):
        if way[0] == 0:
            src_x, dst_x = pl.ds(0, groups), pl.ds(ends, groups)
        elif way[0] > 0:
            src_x, dst_x = pl.ds(last, groups - last), pl.ds(0, groups - last)
        else:
            src_x, dst_x = pl.ds(0, ends), pl.ds(ends + groups, ends)
        src_y, dst_y = y_span(way[1], depth, tall)
        send(edges.at[src_x, src_y], beside.at[0 if way[2] > 0 else 1, dst_x, dst_y], way, 0)

    def send_all(steps):
        for z_side, action in ((False, send_first), (True, send_edges), (False, send_second)):
            for region in regions:
                if z_side == (region[1] != 0):

                    def go(region=region, action=action):
                        for way in ways_of(region, steps):
                            action(way)

                    guard(region, go)

    by_class(send_all)

    def x_rows(step, reach):
        return reach if step else nx

    def y_rows(step, reach):
        return reach if step else ny

    def moved_rows(way, kind):
        if kind == 2:
            return (ends if way[0] else groups) * y_rows(way[1], depth)
        reaches = ((depth, depth - 2), (depth, depth - 1))[kind]
        return sum(x_rows(way[0], r) * y_rows(way[1], r) for r in reaches)

    def region_wait(region, kinds, semaphore, receive):
        def wait(ways):
            rows = sum(moved_rows(way, kind) for way in ways for kind in kinds)
            if rows == 0:
                return
            whole = pltpu.make_async_remote_copy(
                src_ref=ledger.at[pl.ds(0, rows)],
                dst_ref=ledger.at[pl.ds(0, rows)],
                send_sem=semaphore,
                recv_sem=semaphore,
                device_id=all_targets[0],
                device_id_type=MESH,
            )
            if receive:
                whole.wait_recv()
            else:
                whole.wait_send()

        def go():
            wait(ways_of(region, (0,) if counts[1] == 1 else (0, 1)))
            if counts[1] > 2:
                inner = jnp.logical_and(here[1] > 0, here[1] < counts[1] - 1)
                pl.when(inner)(lambda: wait(ways_of((region[0], region[1]), (1,))))

        guard(region, go)

    def wait_halo(kind):
        for region in regions:
            if (kind == 2) == (region[1] != 0):
                stage = 9 if kind == 1 else 0
                region_wait(region, (kind,), halo_recv.at[stage + REGIONS.index(region)], True)

    if direct:
        signal_all(near)
        hops = [(a, 0, c) for a in (0, 2, -2) for c in (0, 2, -2) if a or c]
        hops = [h for h in hops if abs(h[0]) < counts[0] and abs(h[2]) < counts[2]]
        pl.semaphore_wait(near, neighbours())
        for hop in hops:
            signal(far, hop)

    def share(stage, rows_ref, slot, targets):
        for target in targets:
            pltpu.make_async_remote_copy(
                src_ref=row_out.at[stage],
                dst_ref=rows_ref.at[slot],
                send_sem=row_send.at[stage],
                recv_sem=row_recv.at[stage],
                device_id=target,
                device_id_type=MESH,
            ).start()

    def share_wait(stage, rows_ref, targets):
        if targets:
            whole = pltpu.make_async_remote_copy(
                src_ref=rows_ref.at[pl.ds(0, len(targets))],
                dst_ref=rows_ref.at[pl.ds(0, len(targets))],
                send_sem=row_send.at[stage],
                recv_sem=row_recv.at[stage],
                device_id=targets[0],
                device_id_type=MESH,
            )
            whole.wait_send()
            whole.wait_recv()

    wait_halo(0)
    wait_halo(2)

    first_half = lax.broadcasted_iota(jnp.int32, (SUB, LANES), 0) < SUB // 2
    left_side = lax.broadcasted_iota(jnp.int32, (tall, LANES), 1) % SLOT < depth

    def narrow(v):
        mask = jnp.concatenate([first_half] * (v.shape[1] // LANES), axis=1)
        join = jnp.where(mask, v[ny : ny + SUB], v[ny + SUB :])
        return jnp.concatenate([v[:ny], join], axis=0)

    spans = [(0, ends, 0, depth, nx - depth - last * PER)]
    spans += [(ends, groups, depth, nx, 0), (ends + groups, ends, depth + nx, depth, 0)]
    for first_group, some, first_plane, planes, skip in spans:
        for g in range(some):
            merged = jnp.where(left_side, beside[0, first_group + g], beside[1, first_group + g])
            thin = narrow(merged)
            for s in range(PER):
                j = g * PER + s - skip
                if not 0 <= j < planes:
                    continue
                i = first_plane + j
                shifts = [-((s * FIELDS + f) * SLOT + depth) % LANES for f in range(FIELDS)]
                for f in range(2):
                    pair[f, i, :, nz:] = pltpu.roll(merged, shifts[f], 1)
                if 1 <= i < wide - 1:
                    push_in[i, :, nz:] = pltpu.roll(thin, shifts[2], 1)
                if 2 <= i < wide - 2:
                    cool[i, :, nz:] = pltpu.roll(thin, shifts[3], 1)

    def along_x(least, most, planes_of, use):
        before = sums = None
        for i in range(least, most):
            now = planes_of(i)
            if i > least:
                joined = [a + b for a, b in zip(before, now)]
                if sums is not None:
                    use(i - 1, *[a + b for a, b in zip(sums, joined)])
                sums = joined
            before = now

    def ring_of(i):
        return (smooth_z(narrow(smooth_y(pair[1, i]))),)

    def use_ring(i, ring):
        cond = narrow(pair[1, i])
        base = twice * (8.0 * interval_delta * cond + quarter * ring)
        spread[i] = base
        couple[i] = (quarter * twice) * cond
        if 2 <= i < wide - 2:
            diag[i] = base + twice * ((1.0 - middle) + interval_delta * cooling * cool[i])

    along_x(0, wide, ring_of, use_ring)

    wait_halo(1)

    totals = [None] * MOMENTS

    def gather(n, a, b):
        part = a * b
        part = part[:SUB] + part[SUB:] if ny == 2 * SUB else sum(
            part[r : r + SUB] for r in range(0, ny, SUB)
        )
        totals[n] = part if totals[n] is None else totals[n] + part

    def core(v):
        return v[:ny, :nz]

    def warm_of(i):
        warm = pair[0, i]
        warm_flux = (quarter * twice) * (pair[1, i] * warm)
        return smooth_z(narrow(smooth_y(warm))), smooth_z(narrow(smooth_y(warm_flux)))

    def use_warm(i, ring, push):
        edge = couple[i]
        image = spread[i] * narrow(pair[0, i]) - (edge * ring + inside(i) * push)
        fresh = push_in[i] - image
        basis[0, i] = fresh
        flux[0, i] = edge * fresh
        if depth <= i < depth + nx:
            gather(0, core(fresh), core(fresh))

    along_x(0, wide, warm_of, use_warm)

    for k in range(ITERS - 1):

        def level_of(i, k=k):
            return smooth_z(smooth_y(basis[k, i])), smooth_z(smooth_y(flux[k % 2, i]))

        def use_level(i, ring, push, k=k):
            edge = couple[i]
            mid = basis[k, i]
            fresh = diag[i] * mid - (edge * ring + inside(i) * push)
            if k > 0:
                fresh = fresh - basis[k - 1, i]
            basis[k + 1, i] = fresh
            flux[(k + 1) % 2, i] = edge * fresh
            if depth <= i < depth + nx:
                gather(2 * k + 1, core(mid), core(fresh))
                gather(2 * k + 2, core(fresh), core(fresh))

        along_x(k + 1, wide - k - 1, level_of, use_level)

    k = ITERS - 1

    def last_of(i):
        return (
            smooth_z_own(smooth_y(basis[k, i])[:ny]),
            smooth_z_own(smooth_y(flux[k % 2, i])[:ny]),
        )

    def use_last(i, ring, push):
        mid = basis[k, i, 0:ny, 0:nz]
        fresh = diag[i, 0:ny, 0:nz] * mid - (couple[i, 0:ny, 0:nz] * ring + push)
        fresh = fresh - basis[k - 1, i, 0:ny, 0:nz]
        basis[k + 1, i, 0:ny, 0:nz] = fresh
        gather(2 * k + 1, mid, fresh)

    along_x(depth - 1, depth + nx + 1, last_of, use_last)

    diagonal = lax.broadcasted_iota(jnp.int32, (SUB, LANES), 0)
    across = lax.broadcasted_iota(jnp.int32, (SUB, LANES), 1)
    tile = jnp.zeros((SUB, LANES), jnp.float32)
    for n in range(MOMENTS):
        tile = jnp.where(diagonal == n, jnp.sum(totals[n], axis=0, keepdims=True), tile)
    column = jnp.sum(tile, axis=1, keepdims=True)
    row = jnp.sum(jnp.where(across == diagonal, column, 0.0), axis=0, keepdims=True)
    if direct:
        pl.semaphore_wait(far, present(back(h) for h in hops))
    row_out[0] = row

    def settle():
        for region in regions:
            kinds = (2,) if region[1] else (0, 1)
            region_wait(region, kinds, halo_send.at[REGIONS.index(region)], False)

    if direct:
        mine = in_plane * line + here[2]
        all_rows[mine] = row
        share(0, all_rows, mine, all_targets)
        settle()
        share_wait(0, all_rows, all_targets)
        row = jnp.sum(all_rows[...], axis=0)
    else:
        plane_rows[in_plane] = row
        share(0, plane_rows, in_plane, plane_targets)
        settle()
        share_wait(0, plane_rows, plane_targets)
        row = jnp.sum(plane_rows[...], axis=0)
        row_out[1] = row
        line_rows[here[2]] = row
        share(1, line_rows, here[2], line_targets)
        share_wait(1, line_rows, line_targets)
        row = jnp.sum(line_rows[...], axis=0)
    row_lane = lax.broadcasted_iota(jnp.int32, (1, LANES), 1)
    gram = {}
    for n in range(MOMENTS):
        value = jnp.sum(jnp.where(row_lane == n, row, 0.0), axis=1, keepdims=True)
        gram[n // 2, (n + 1) // 2] = value
    for gap in range(2, ITERS + 1):
        for i in range(ITERS + 1 - gap):
            j = i + gap
            value = gram[i + 1, j - 1] - gram[i, j - 2]
            if i > 0:
                value = value + gram[i - 1, j - 1]
            gram[i, j] = value
    for i, j in list(gram):
        gram[j, i] = gram[i, j]

    def apply(p):
        q = [middle * a for a in p] + [jnp.zeros_like(half)]
        for i, a in enumerate(p):
            q[i + 1] = q[i + 1] + (0.5 * half) * a
            if i > 0:
                q[i - 1] = q[i - 1] + (0.5 * half) * a
        return q

    def product(p, q):
        value = None
        for i, a in enumerate(p):
            inner = None
            for j, b in enumerate(q):
                term = gram[i, j] * b
                inner = term if inner is None else inner + term
            inner = a * inner
            value = inner if value is None else value + inner
        return value

    left = [0.5 * half]
    heading = list(left)
    moved = []
    norm = product(left, left)
    for step in range(ITERS):
        image = apply(heading)
        alpha = norm / product(heading, image)
        moved = [a + alpha * b for a, b in zip(moved, heading)] + [
            alpha * b for b in heading[len(moved) :]
        ]
        left = [a - alpha * b for a, b in zip(left, image)] + [
            -alpha * b for b in image[len(left) :]
        ]
        if step + 1 < ITERS:
            following = product(left, left)
            ratio = following / norm
            heading = [a + ratio * b for a, b in zip(left, heading)] + left[len(heading) :]
            norm = following

    for i in range(nx):
        warm = pair[0, depth + i, 0:ny, 0:nz]
        end = jnp.zeros_like(warm)
        for k in range(ITERS + 1):
            value = basis[k, depth + i, 0:ny, 0:nz]
            if k < ITERS:
                warm = warm + moved[k] * value
            end = end + left[k] * value
        both_out[0, i] = warm
        both_out[1, i] = end


def body(counts, warm, source, category, table, flags):
    nx, ny, nz = warm.shape
    depth = DEPTH
    groups, ends = -(-nx // PER), -(-depth // PER)
    plane, line = counts[0] * counts[1], counts[2]
    if nx < depth or nx % 2 or ny % SUB or nz != LANES or table.shape[0] > LANES:
        raise ValueError("block shape")
    if groups - (nx - depth) // PER != ends:
        raise ValueError("block shape")
    wide, tall, short, long = nx + 2 * depth, ny + 2 * SUB, ny + SUB, nz + LANES
    table = table[None]
    any_spec = pl.BlockSpec(memory_space=pl.ANY)
    vmem = pl.BlockSpec(memory_space=pltpu.VMEM)
    f32 = jnp.float32
    both = pl.pallas_call(
        functools.partial(kernel, counts),
        out_shape=pltpu.VMEM((2,) + warm.shape, jnp.float32),
        in_specs=[any_spec] * 5,
        out_specs=vmem,
        scratch_shapes=[
            pltpu.VMEM((2, wide, tall, long), f32),
            pltpu.VMEM((wide, short, long), f32),
            pltpu.VMEM((wide, short, long), f32),
            pltpu.VMEM((ITERS + 1, wide, short, long), f32),
            pltpu.VMEM((2, wide, short, long), f32),
            pltpu.VMEM((wide, short, long), f32),
            pltpu.VMEM((wide, short, long), f32),
            pltpu.VMEM((wide, short, long), f32),
            pltpu.VMEM((3, short, long), f32),
            pltpu.VMEM((SUB, LANES), f32),
            pltpu.VMEM(table.shape, f32),
            pltpu.VMEM((nx, ny, nz), f32),
            pltpu.VMEM((2, nx, ny, nz), jnp.int32),
            pltpu.VMEM((groups, ny, nz), f32),
            pltpu.VMEM((2, groups + 2 * ends, tall, nz), f32),
            pltpu.VMEM((4 * nx * ny, LANES), f32),
            pltpu.VMEM((2, 1, LANES), f32),
            pltpu.VMEM((plane, 1, LANES), f32),
            pltpu.VMEM((line, 1, LANES), f32),
            pltpu.VMEM((plane * line, 1, LANES), f32),
            pltpu.SemaphoreType.DMA((2,)),
            pltpu.SemaphoreType.DMA((9,)),
            pltpu.SemaphoreType.DMA((12,)),
            pltpu.SemaphoreType.DMA((2,)),
            pltpu.SemaphoreType.DMA((2,)),
            pltpu.SemaphoreType.REGULAR,
            pltpu.SemaphoreType.REGULAR,
        ],
        compiler_params=pltpu.CompilerParams(collective_id=0, has_side_effects=True),
    )(warm, source, category, table, flags)
    return both[0], both[1]


def solution(mesh):
    counts = tuple(mesh.shape[a] for a in AXES)
    spec = P("gx", "gy", "gz")
    return jax.shard_map(
        functools.partial(body, counts),
        mesh=mesh,
        in_specs=(spec, spec, spec, P(), spec),
        out_specs=(spec, spec),
        check_vma=False,
    )
```

time: 21.2 us -> 18.8 us (0.89)
  Pallas kernels: 19.7 us -> 17.3 us
    pallas_call x1, Pallas kernels: 19.7 us -> 17.3 us  [body(): pl.pallas_call(functools.partial(kernel, counts), out_shape=pltpu.VMEM((2...]
where the time goes in v2:
time: 18.8 us; the launch traced here: 18.6 us
  Pallas kernels  17.3 us (92%)
  local copies, waits for them, and re-layouts  0.66 us (4%)
  between operations  0.64 us (3%)
    pallas_call x1, Pallas kernels, body(): pl.pallas_call(functools.partial(kernel, counts), out_shape=pltpu.VMEM((2...  17.3 us
    squeeze x1, local copies, waits for them, and re-layouts, body(): return (both[0], both[1])  0.66 us

profile of v2, /device:TPU:0, one launch (start us, length us, event | category | flops | bytes accessed | tf_op | source)
XLA Modules:
  0.0 18.6 jit_solution(14375569698382493210)
XLA Ops:
  0.6 17.3 %shard_map.68 = f32[2,8,16,128]{3,2,1,0:T(8,128)S(1)} custom-call(f32[8,16,128]{2,1,0:T(8,128)} %warm_in.1, f32[8,16,128]{2,1,0:T(8,128)} %source_in.1, s32[8,16,128]{2,1,0:T(8,128)} %category_in.1, f32[1,16]{1,0:T(1,128)} %bitcast.5, s32[8,16,128]{2,1,0:T(8,128)} %flags_in.1), custom_call_target="tpu_custom_call" | custom-call | tf_op jit(solution)/shard_map/pallas_call | solution.py:658
  18.0 0.7 %slice_bitcast_fusion = (f32[8,16,128]{2,1,0:T(8,128)}, f32[8,16,128]{2,1,0:T(8,128)}) fusion(f32[2,8,16,128]{3,2,1,0:T(8,128)S(1)} %shard_map.68), kind=kLoop, calls=%fused_computation | loop fusion | bytes 262144 | tf_op jit(solution)/shard_map/squeeze | solution.py:694

commit v3 on v2

--- a/solution.py
+++ b/solution.py
@@ -18,8 +18,7 @@
 LANES = 128
 FIELDS = 4
 DEPTH = ITERS + 1
-SLOT = 2 * DEPTH
-PER = LANES // (FIELDS * SLOT)
+BOTH = 2
 MOMENTS = 2 * ITERS
 REGIONS = [(a, c) for c in (0, 1, -1) for a in (0, 1, -1)]
 
@@ -84,9 +83,7 @@
     depth = DEPTH
     wide, tall, long = pair.shape[1:]
     short = ny + SUB
-    groups = edges.shape[0]
-    ends = -(-depth // PER)
-    last = (nx - depth) // PER
+    tail = nx - depth
     direct = max(counts) <= REACH
     here = [lax.axis_index(a) for a in AXES]
     in_plane = here[0] * counts[1] + here[1]
@@ -199,8 +196,8 @@
     table[...] = jnp.zeros(table.shape, jnp.float32)
     body = slice(0, nz)
     for way, planes, slots in (
-        ((-1, 0, 0), slice(0, depth), slice(0, ends)),
-        ((1, 0, 0), slice(depth + nx, wide), slice(ends + groups, None)),
+        ((-1, 0, 0), slice(0, depth), 0),
+        ((1, 0, 0), slice(depth + nx, wide), 1 + BOTH),
     ):
 
         @pl.when(jnp.logical_not(exists(way)))
@@ -262,22 +259,32 @@
 
     every = ledger.at[pl.ds(0, 4 * nx * ny)]
     pltpu.make_async_copy(every, every, load_sems.at[1]).wait()
-    for start in range(0, nx, PER):
-        packed = None
-        for i in range(start, min(start + PER, nx)):
-            cond = jnp.take_along_axis(lookup, ints[0, i], axis=1)
-            flag = ints[1, i].astype(jnp.float32)
-            warm = pair[0, depth + i, 0:ny, 0:nz]
-            push = interval_delta * source[i] - (interval_delta * cooling) * flag * warm
-            push = twice * push
-            pair[1, depth + i, 0:ny, 0:nz] = cond
-            cool[depth + i, 0:ny, 0:nz] = flag
-            push_in[depth + i, 0:ny, 0:nz] = push
+    packed = [[None, None], [None, None]]
+    for i in range(nx):
+        cond = jnp.take_along_axis(lookup, ints[0, i], axis=1)
+        flag = ints[1, i].astype(jnp.float32)
+        warm = pair[0, depth + i, 0:ny, 0:nz]
+        push = interval_delta * source[i] - (interval_delta * cooling) * flag * warm
+        push = twice * push
+        pair[1, depth + i, 0:ny, 0:nz] = cond
+        cool[depth + i, 0:ny, 0:nz] = flag
+        push_in[depth + i, 0:ny, 0:nz] = push
+        for g, start in enumerate((0, tail)):
+            if not 0 <= i - start < depth:
+                continue
             for f, piece in enumerate((warm, cond, push, flag)):
-                q = (i - start) * FIELDS + f
-                turned = pltpu.roll(piece, (q * SLOT + depth) % LANES, 1)
-                packed = turned if packed is None else jnp.where(lane >= q * SLOT, turned, packed)
-        edges[start // PER] = packed
+                at_lane = ((i - start) * FIELDS + f) * depth
+                turned = pltpu.roll(piece, at_lane + depth, 1)
+                for side in range(2):
+                    old = packed[side][g]
+                    if old is not None:
+                        turned_in = jnp.where(lane >= at_lane + side * depth, turned, old)
+                    else:
+                        turned_in = turned
+                    packed[side][g] = turned_in
+    for side in range(2):
+        for g in range(BOTH):
+            edges[side, g] = packed[side][g]
 
     waits = neighbours()
     if not direct:
@@ -299,12 +306,11 @@
         return pl.ds(depth, reach), pl.ds(depth + nx, reach)
 
     def send(src, dst, way, stage):
-        region = (way[0], way[2])
         pltpu.make_async_remote_copy(
             src_ref=src,
             dst_ref=dst,
-            send_sem=halo_send.at[REGIONS.index(region)],
-            recv_sem=halo_recv.at[stage + REGIONS.index((-way[0], -way[2]))],
+            send_sem=halo_send.at[0],
+            recv_sem=halo_recv.at[stage],
             device_id=at(way),
             device_id_type=MESH,
         ).start()
@@ -320,29 +326,39 @@
         send_field(lambda *v: cool.at[v], way, depth - 2, short, 0)
 
     def send_second(way):
-        send_field(lambda *v: pair.at[(0,) + v], way, depth, tall, 9)
-        send_field(lambda *v: push_in.at[v], way, depth - 1, short, 9)
+        send_field(lambda *v: pair.at[(0,) + v], way, depth, tall, 1)
+        send_field(lambda *v: push_in.at[v], way, depth - 1, short, 1)
 
     def send_edges(way):
         if way[0] == 0:
-            src_x, dst_x = pl.ds(0, groups), pl.ds(ends, groups)
+            src_x, dst_x = pl.ds(0, BOTH), pl.ds(1, BOTH)
         elif way[0] > 0:
-            src_x, dst_x = pl.ds(last, groups - last), pl.ds(0, groups - last)
+            src_x, dst_x = pl.ds(1, 1), pl.ds(0, 1)
         else:
-            src_x, dst_x = pl.ds(0, ends), pl.ds(ends + groups, ends)
+            src_x, dst_x = pl.ds(0, 1), pl.ds(1 + BOTH, 1)
         src_y, dst_y = y_span(way[1], depth, tall)
-        send(edges.at[src_x, src_y], beside.at[0 if way[2] > 0 else 1, dst_x, dst_y], way, 0)
+        side = 0 if way[2] > 0 else 1
+        send(edges.at[side, src_x, src_y], beside.at[side, dst_x, dst_y], way, 0)
 
     def send_all(steps):
-        for z_side, action in ((False, send_first), (True, send_edges), (False, send_second)):
-            for region in regions:
-                if z_side == (region[1] != 0):
-
-                    def go(region=region, action=action):
-                        for way in ways_of(region, steps):
-                            action(way)
-
-                    guard(region, go)
+        steps_on = tuple(v for v in steps if v)
+        sides = [r for r in regions if r[0] and not r[1]]
+        depths = sorted([r for r in regions if r[1]], key=lambda r: -abs(r[0]))
+        plan = [(r, steps, (send_edges,)) for r in depths]
+        plan += [(r, steps_on, (send_first,)) for r in sides]
+        for action in (send_first, send_second):
+            if action is send_second:
+                plan += [(r, steps_on, (action,)) for r in sides]
+            plan += [((0, 0), steps_on, (action,))] + [(r, (0,), (action,)) for r in sides]
+        for region, some, actions in plan:
+
+            def go(region=region, some=some, actions=actions):
+                for action in actions:
+                    for way in ways_of(region, some):
+                        action(way)
+
+            if ways_of(region, some):
+                guard(region, go)
 
     by_class(send_all)
 
@@ -354,13 +370,28 @@
 
     def moved_rows(way, kind):
         if kind == 2:
-            return (ends if way[0] else groups) * y_rows(way[1], depth)
+            return (1 if way[0] else BOTH) * y_rows(way[1], depth)
         reaches = ((depth, depth - 2), (depth, depth - 1))[kind]
         return sum(x_rows(way[0], r) * y_rows(way[1], r) for r in reaches)
 
-    def region_wait(region, kinds, semaphore, receive):
-        def wait(ways):
-            rows = sum(moved_rows(way, kind) for way in ways for kind in kinds)
+    def sides_of(k):
+        if counts[k] == 1:
+            return [(None, 0)]
+        edge = jnp.logical_or(here[k] == 0, here[k] == counts[k] - 1)
+        if counts[k] == 2:
+            return [(None, 1)]
+        return [(edge, 1), (jnp.logical_not(edge), 2)]
+
+    def wait_all(kinds, semaphore, receive):
+        def wait(sides):
+            rows = 0
+            for way in [(a, b, c) for a in (0, 1) for b in (0, 1) for c in (0, 1)]:
+                times = 1
+                for step, some in zip(way, sides):
+                    times = times * (some if step else 1)
+                for kind in kinds:
+                    if any(way) and (kind == 2) == bool(way[2]):
+                        rows = rows + times * moved_rows(way, kind)
             if rows == 0:
                 return
             whole = pltpu.make_async_remote_copy(
@@ -376,19 +407,18 @@
             else:
                 whole.wait_send()
 
-        def go():
-            wait(ways_of(region, (0,) if counts[1] == 1 else (0, 1)))
-            if counts[1] > 2:
-                inner = jnp.logical_and(here[1] > 0, here[1] < counts[1] - 1)
-                pl.when(inner)(lambda: wait(ways_of((region[0], region[1]), (1,))))
-
-        guard(region, go)
-
-    def wait_halo(kind):
-        for region in regions:
-            if (kind == 2) == (region[1] != 0):
-                stage = 9 if kind == 1 else 0
-                region_wait(region, (kind,), halo_recv.at[stage + REGIONS.index(region)], True)
+        for x_good, x_some in sides_of(0):
+            for y_good, y_some in sides_of(1):
+                for z_good, z_some in sides_of(2):
+                    good = None
+                    for one in (x_good, y_good, z_good):
+                        if one is not None:
+                            good = one if good is None else jnp.logical_and(good, one)
+                    act = functools.partial(wait, (x_some, y_some, z_some))
+                    if good is None:
+                        act()
+                    else:
+                        pl.when(good)(act)
 
     if direct:
         signal_all(near)
@@ -422,35 +452,34 @@
             whole.wait_send()
             whole.wait_recv()
 
-    wait_halo(0)
-    wait_halo(2)
+    wait_all((0, 2), halo_recv.at[0], True)
 
     first_half = lax.broadcasted_iota(jnp.int32, (SUB, LANES), 0) < SUB // 2
-    left_side = lax.broadcasted_iota(jnp.int32, (tall, LANES), 1) % SLOT < depth
+    tall_lane = lax.broadcasted_iota(jnp.int32, (tall, LANES), 1)
 
     def narrow(v):
         mask = jnp.concatenate([first_half] * (v.shape[1] // LANES), axis=1)
         join = jnp.where(mask, v[ny : ny + SUB], v[ny + SUB :])
         return jnp.concatenate([v[:ny], join], axis=0)
 
-    spans = [(0, ends, 0, depth, nx - depth - last * PER)]
-    spans += [(ends, groups, depth, nx, 0), (ends + groups, ends, depth + nx, depth, 0)]
-    for first_group, some, first_plane, planes, skip in spans:
-        for g in range(some):
-            merged = jnp.where(left_side, beside[0, first_group + g], beside[1, first_group + g])
-            thin = narrow(merged)
-            for s in range(PER):
-                j = g * PER + s - skip
-                if not 0 <= j < planes:
-                    continue
-                i = first_plane + j
-                shifts = [-((s * FIELDS + f) * SLOT + depth) % LANES for f in range(FIELDS)]
-                for f in range(2):
-                    pair[f, i, :, nz:] = pltpu.roll(merged, shifts[f], 1)
-                if 1 <= i < wide - 1:
-                    push_in[i, :, nz:] = pltpu.roll(thin, shifts[2], 1)
-                if 2 <= i < wide - 2:
-                    cool[i, :, nz:] = pltpu.roll(thin, shifts[3], 1)
+    places = [(0, j) for j in range(depth)]
+    places += [(1, p) if p < depth else (2, p - tail) for p in range(nx)]
+    places += [(1 + BOTH, j) for j in range(depth)]
+    for i, (g, slot) in enumerate(places):
+        full = [beside[side, g] for side in range(2)]
+        thin = [narrow(v) for v in full]
+        for f, ref in enumerate((pair, pair, push_in, cool)):
+            spare = (0, 0, 1, 2)[f]
+            if not spare <= i < wide - spare:
+                continue
+            cut = (slot * FIELDS + f + 1) * depth
+            both = full if f < 2 else thin
+            kept = jnp.where(tall_lane[: both[0].shape[0]] < cut, both[0], both[1])
+            kept = pltpu.roll(kept, LANES - cut, 1)
+            if f < 2:
+                ref[f, i, :, nz:] = kept
+            else:
+                ref[i, :, nz:] = kept
 
     def along_x(least, most, planes_of, use):
         before = sums = None
@@ -476,7 +505,7 @@
 
     along_x(0, wide, ring_of, use_ring)
 
-    wait_halo(1)
+    wait_all((1,), halo_recv.at[1], True)
 
     totals = [None] * MOMENTS
 
@@ -554,9 +583,7 @@
     row_out[0] = row
 
     def settle():
-        for region in regions:
-            kinds = (2,) if region[1] else (0, 1)
-            region_wait(region, kinds, halo_send.at[REGIONS.index(region)], False)
+        wait_all((0, 1, 2), halo_send.at[0], False)
 
     if direct:
         mine = in_plane * line + here[2]
@@ -644,11 +671,10 @@
 def body(counts, warm, source, category, table, flags):
     nx, ny, nz = warm.shape
     depth = DEPTH
-    groups, ends = -(-nx // PER), -(-depth // PER)
     plane, line = counts[0] * counts[1], counts[2]
     if nx < depth or nx % 2 or ny % SUB or nz != LANES or table.shape[0] > LANES:
         raise ValueError("block shape")
-    if groups - (nx - depth) // PER != ends:
+    if nx > 2 * depth or (FIELDS * depth + 1) * depth > LANES:
         raise ValueError("block shape")
     wide, tall, short, long = nx + 2 * depth, ny + 2 * SUB, ny + SUB, nz + LANES
     table = table[None]
@@ -674,16 +700,16 @@
             pltpu.VMEM(table.shape, f32),
             pltpu.VMEM((nx, ny, nz), f32),
             pltpu.VMEM((2, nx, ny, nz), jnp.int32),
-            pltpu.VMEM((groups, ny, nz), f32),
-            pltpu.VMEM((2, groups + 2 * ends, tall, nz), f32),
-            pltpu.VMEM((4 * nx * ny, LANES), f32),
+            pltpu.VMEM((2, BOTH, ny, nz), f32),
+            pltpu.VMEM((2, BOTH + 2, tall, nz), f32),
+            pltpu.VMEM((16 * nx * ny, LANES), f32),
             pltpu.VMEM((2, 1, LANES), f32),
             pltpu.VMEM((plane, 1, LANES), f32),
             pltpu.VMEM((line, 1, LANES), f32),
             pltpu.VMEM((plane * line, 1, LANES), f32),
             pltpu.SemaphoreType.DMA((2,)),
-            pltpu.SemaphoreType.DMA((9,)),
-            pltpu.SemaphoreType.DMA((12,)),
+            pltpu.SemaphoreType.DMA((1,)),
+            pltpu.SemaphoreType.DMA((2,)),
             pltpu.SemaphoreType.DMA((2,)),
             pltpu.SemaphoreType.DMA((2,)),
             pltpu.SemaphoreType.REGULAR,

time: 18.8 us -> 18.6 us (0.989)
  Pallas kernels: 17.3 us -> 17.1 us
    pallas_call x1, Pallas kernels: 17.3 us -> 17.1 us  [body(): pl.pallas_call(functools.partial(kernel, counts), out_shape=pltpu.VMEM((2...]
where the time goes in v3:
time: 18.6 us; the launch traced here: 18.4 us
  Pallas kernels  17.1 us (92%)
  local copies, waits for them, and re-layouts  0.66 us (4%)
  between operations  0.64 us (3%)
    pallas_call x1, Pallas kernels, body(): pl.pallas_call(functools.partial(kernel, counts), out_shape=pltpu.VMEM((2...  17.1 us
    squeeze x1, local copies, waits for them, and re-layouts, body(): return (both[0], both[1])  0.66 us

profile of v3, /device:TPU:0, one launch (start us, length us, event | category | flops | bytes accessed | tf_op | source)
XLA Modules:
  0.0 18.4 jit_solution(12402782560957759578)
XLA Ops:
  0.6 17.1 %shard_map.68 = f32[2,8,16,128]{3,2,1,0:T(8,128)S(1)} custom-call(f32[8,16,128]{2,1,0:T(8,128)} %warm_in.1, f32[8,16,128]{2,1,0:T(8,128)} %source_in.1, s32[8,16,128]{2,1,0:T(8,128)} %category_in.1, f32[1,16]{1,0:T(1,128)} %bitcast.5, s32[8,16,128]{2,1,0:T(8,128)} %flags_in.1), custom_call_target="tpu_custom_call" | custom-call | tf_op jit(solution)/shard_map/pallas_call | solution.py:684
  17.7 0.7 %slice_bitcast_fusion = (f32[8,16,128]{2,1,0:T(8,128)}, f32[8,16,128]{2,1,0:T(8,128)}) fusion(f32[2,8,16,128]{3,2,1,0:T(8,128)S(1)} %shard_map.68), kind=kLoop, calls=%fused_computation | loop fusion | bytes 262144 | tf_op jit(solution)/shard_map/squeeze | solution.py:720

commit v4 on v3

--- a/solution.py
+++ b/solution.py
@@ -54,7 +54,6 @@
     push_in,
     cool,
     basis,
-    flux,
     spread,
     diag,
     couple,
@@ -321,13 +320,15 @@
         z = pl.ds(0, nz)
         send(view(src_x, src_y, z), view(dst_x, dst_y, z), way, stage)
 
-    def send_first(way):
+    def send_cond(way):
         send_field(lambda *v: pair.at[(1,) + v], way, depth, tall, 0)
-        send_field(lambda *v: cool.at[v], way, depth - 2, short, 0)
-
-    def send_second(way):
+
+    def send_warm(way):
         send_field(lambda *v: pair.at[(0,) + v], way, depth, tall, 1)
-        send_field(lambda *v: push_in.at[v], way, depth - 1, short, 1)
+
+    def send_rest(way):
+        send_field(lambda *v: push_in.at[v], way, depth - 1, short, 2)
+        send_field(lambda *v: cool.at[v], way, depth - 2, short, 2)
 
     def send_edges(way):
         if way[0] == 0:
@@ -345,11 +346,8 @@
         sides = [r for r in regions if r[0] and not r[1]]
         depths = sorted([r for r in regions if r[1]], key=lambda r: -abs(r[0]))
         plan = [(r, steps, (send_edges,)) for r in depths]
-        plan += [(r, steps_on, (send_first,)) for r in sides]
-        for action in (send_first, send_second):
-            if action is send_second:
-                plan += [(r, steps_on, (action,)) for r in sides]
-            plan += [((0, 0), steps_on, (action,))] + [(r, (0,), (action,)) for r in sides]
+        for action in (send_cond, send_warm, send_rest):
+            plan += [((0, 0), steps_on, (action,))] + [(r, steps, (action,)) for r in sides]
         for region, some, actions in plan:
 
             def go(region=region, some=some, actions=actions):
@@ -369,9 +367,9 @@
         return reach if step else ny
 
     def moved_rows(way, kind):
-        if kind == 2:
+        if kind == 3:
             return (1 if way[0] else BOTH) * y_rows(way[1], depth)
-        reaches = ((depth, depth - 2), (depth, depth - 1))[kind]
+        reaches = ((depth,), (depth,), (depth - 1, depth - 2))[kind]
         return sum(x_rows(way[0], r) * y_rows(way[1], r) for r in reaches)
 
     def sides_of(k):
@@ -390,7 +388,7 @@
                 for step, some in zip(way, sides):
                     times = times * (some if step else 1)
                 for kind in kinds:
-                    if any(way) and (kind == 2) == bool(way[2]):
+                    if any(way) and (kind == 3) == bool(way[2]):
                         rows = rows + times * moved_rows(way, kind)
             if rows == 0:
                 return
@@ -452,7 +450,7 @@
             whole.wait_send()
             whole.wait_recv()
 
-    wait_all((0, 2), halo_recv.at[0], True)
+    wait_all((0, 3), halo_recv.at[0], True)
 
     first_half = lax.broadcasted_iota(jnp.int32, (SUB, LANES), 0) < SUB // 2
     tall_lane = lax.broadcasted_iota(jnp.int32, (tall, LANES), 1)
@@ -465,21 +463,25 @@
     places = [(0, j) for j in range(depth)]
     places += [(1, p) if p < depth else (2, p - tail) for p in range(nx)]
     places += [(1 + BOTH, j) for j in range(depth)]
-    for i, (g, slot) in enumerate(places):
-        full = [beside[side, g] for side in range(2)]
-        thin = [narrow(v) for v in full]
-        for f, ref in enumerate((pair, pair, push_in, cool)):
-            spare = (0, 0, 1, 2)[f]
-            if not spare <= i < wide - spare:
-                continue
-            cut = (slot * FIELDS + f + 1) * depth
-            both = full if f < 2 else thin
-            kept = jnp.where(tall_lane[: both[0].shape[0]] < cut, both[0], both[1])
-            kept = pltpu.roll(kept, LANES - cut, 1)
-            if f < 2:
-                ref[f, i, :, nz:] = kept
-            else:
-                ref[i, :, nz:] = kept
+
+    def unpack(fields):
+        for i, (g, slot) in enumerate(places):
+            both = [beside[side, g] for side in range(2)]
+            if fields[0] >= 2:
+                both = [narrow(v) for v in both]
+            for f in fields:
+                ref, spare = ((pair, 0), (pair, 0), (push_in, 1), (cool, 2))[f]
+                if not spare <= i < wide - spare:
+                    continue
+                cut = (slot * FIELDS + f + 1) * depth
+                kept = jnp.where(tall_lane[: both[0].shape[0]] < cut, both[0], both[1])
+                kept = pltpu.roll(kept, LANES - cut, 1)
+                if f < 2:
+                    ref[f, i, :, nz:] = kept
+                else:
+                    ref[i, :, nz:] = kept
+
+    unpack((1, 0))
 
     def along_x(least, most, planes_of, use):
         before = sums = None
@@ -500,8 +502,6 @@
         base = twice * (8.0 * interval_delta * cond + quarter * ring)
         spread[i] = base
         couple[i] = (quarter * twice) * cond
-        if 2 <= i < wide - 2:
-            diag[i] = base + twice * ((1.0 - middle) + interval_delta * cooling * cool[i])
 
     along_x(0, wide, ring_of, use_ring)
 
@@ -527,27 +527,36 @@
     def use_warm(i, ring, push):
         edge = couple[i]
         image = spread[i] * narrow(pair[0, i]) - (edge * ring + inside(i) * push)
-        fresh = push_in[i] - image
-        basis[0, i] = fresh
-        flux[0, i] = edge * fresh
-        if depth <= i < depth + nx:
-            gather(0, core(fresh), core(fresh))
+        basis[0, i] = image
 
     along_x(0, wide, warm_of, use_warm)
+    unpack((2, 3))
+
+    wait_all((2,), halo_recv.at[2], True)
 
     for k in range(ITERS - 1):
 
         def level_of(i, k=k):
-            return smooth_z(smooth_y(basis[k, i])), smooth_z(smooth_y(flux[k % 2, i]))
+            mid = basis[k, i]
+            if k == 0:
+                mid = push_in[i] - mid
+                basis[0, i] = mid
+                if depth <= i < depth + nx:
+                    gather(0, core(mid), core(mid))
+            return smooth_z(smooth_y(mid)), smooth_z(smooth_y(couple[i] * mid))
 
         def use_level(i, ring, push, k=k):
             edge = couple[i]
             mid = basis[k, i]
-            fresh = diag[i] * mid - (edge * ring + inside(i) * push)
+            if k == 0:
+                main = spread[i] + twice * ((1.0 - middle) + interval_delta * cooling * cool[i])
+                diag[i] = main
+            else:
+                main = diag[i]
+            fresh = main * mid - (edge * ring + inside(i) * push)
             if k > 0:
                 fresh = fresh - basis[k - 1, i]
             basis[k + 1, i] = fresh
-            flux[(k + 1) % 2, i] = edge * fresh
             if depth <= i < depth + nx:
                 gather(2 * k + 1, core(mid), core(fresh))
                 gather(2 * k + 2, core(fresh), core(fresh))
@@ -559,7 +568,7 @@
     def last_of(i):
         return (
             smooth_z_own(smooth_y(basis[k, i])[:ny]),
-            smooth_z_own(smooth_y(flux[k % 2, i])[:ny]),
+            smooth_z_own(smooth_y(couple[i] * basis[k, i])[:ny]),
         )
 
     def use_last(i, ring, push):
@@ -583,7 +592,7 @@
     row_out[0] = row
 
     def settle():
-        wait_all((0, 1, 2), halo_send.at[0], False)
+        wait_all((0, 1, 2, 3), halo_send.at[0], False)
 
     if direct:
         mine = in_plane * line + here[2]
@@ -691,7 +700,6 @@
             pltpu.VMEM((wide, short, long), f32),
             pltpu.VMEM((wide, short, long), f32),
             pltpu.VMEM((ITERS + 1, wide, short, long), f32),
-            pltpu.VMEM((2, wide, short, long), f32),
             pltpu.VMEM((wide, short, long), f32),
             pltpu.VMEM((wide, short, long), f32),
             pltpu.VMEM((wide, short, long), f32),
@@ -709,7 +717,7 @@
             pltpu.VMEM((plane * line, 1, LANES), f32),
             pltpu.SemaphoreType.DMA((2,)),
             pltpu.SemaphoreType.DMA((1,)),
-            pltpu.SemaphoreType.DMA((2,)),
+            pltpu.SemaphoreType.DMA((3,)),
             pltpu.SemaphoreType.DMA((2,)),
             pltpu.SemaphoreType.DMA((2,)),
             pltpu.SemaphoreType.REGULAR,

time: 18.6 us -> 18.1 us (0.973)
  Pallas kernels: 17.1 us -> 16.6 us
    pallas_call x1, Pallas kernels: 17.1 us -> 16.6 us  [body(): pl.pallas_call(functools.partial(kernel, counts), out_shape=pltpu.VMEM((2...]
where the time goes in v4:
time: 18.1 us; the launch traced here: 17.9 us
  Pallas kernels  16.6 us (92%)
  local copies, waits for them, and re-layouts  0.66 us (4%)
  between operations  0.64 us (4%)
    pallas_call x1, Pallas kernels, body(): pl.pallas_call(functools.partial(kernel, counts), out_shape=pltpu.VMEM((2...  16.6 us
    squeeze x1, local copies, waits for them, and re-layouts, body(): return (both[0], both[1])  0.66 us

profile of v4, /device:TPU:0, one launch (start us, length us, event | category | flops | bytes accessed | tf_op | source)
XLA Modules:
  0.0 17.9 jit_solution(7684673903767311002)
XLA Ops:
  0.6 16.6 %shard_map.68 = f32[2,8,16,128]{3,2,1,0:T(8,128)S(1)} custom-call(f32[8,16,128]{2,1,0:T(8,128)} %warm_in.1, f32[8,16,128]{2,1,0:T(8,128)} %source_in.1, s32[8,16,128]{2,1,0:T(8,128)} %category_in.1, f32[1,16]{1,0:T(1,128)} %bitcast.5, s32[8,16,128]{2,1,0:T(8,128)} %flags_in.1), custom_call_target="tpu_custom_call" | custom-call | tf_op jit(solution)/shard_map/pallas_call | solution.py:693
  17.3 0.7 %slice_bitcast_fusion = (f32[8,16,128]{2,1,0:T(8,128)}, f32[8,16,128]{2,1,0:T(8,128)}) fusion(f32[2,8,16,128]{3,2,1,0:T(8,128)S(1)} %shard_map.68), kind=kLoop, calls=%fused_computation | loop fusion | bytes 262144 | tf_op jit(solution)/shard_map/squeeze | solution.py:728

commit v5 on v4

--- a/solution.py
+++ b/solution.py
@@ -23,9 +23,21 @@
 REGIONS = [(a, c) for c in (0, 1, -1) for a in (0, 1, -1)]
 
 
+def tiles_of(values):
+    return [values[r : r + SUB] for r in range(0, values.shape[0], SUB)]
+
+
 def smooth_y(values):
-    pairs = values + pltpu.roll(values, 1, 0)
-    return pairs + pltpu.roll(pairs, values.shape[0] - 1, 0)
+    tiles = tiles_of(values)
+    after = tiles[1:] + [pltpu.roll(tiles[0], SUB - 1, 0)]
+    pairs = [a + b for a, b in zip(tiles, after)]
+    before = [pltpu.roll(pairs[-1], 1, 0)] + pairs[:-1]
+    return jnp.concatenate([a + b for a, b in zip(before, pairs)], axis=0)
+
+
+def smooth_rows(pieces):
+    pairs = [a + b for a, b in zip(pieces, pieces[1:])]
+    return jnp.concatenate([a + b for a, b in zip(pairs, pairs[1:])], axis=0)
 
 
 def smooth_z(values):
@@ -51,13 +63,19 @@
     flags_in,
     both_out,
     pair,
+    side_pair,
     push_in,
     cool,
+    side_push,
+    side_cool,
     basis,
     spread,
     diag,
     couple,
     masks,
+    row_mask,
+    natural,
+    natural_own,
     table,
     table_row,
     source,
@@ -80,8 +98,10 @@
     plane, line = counts[0] * counts[1], counts[2]
     nx, ny, nz = both_out.shape[1:]
     depth = DEPTH
-    wide, tall, long = pair.shape[1:]
+    wide, tall = pair.shape[1:3]
+    long = 2 * nz
     short = ny + SUB
+    leap = short // SUB
     tail = nx - depth
     direct = max(counts) <= REACH
     here = [lax.axis_index(a) for a in AXES]
@@ -120,13 +140,31 @@
     line_targets = [
         {"gx": here[0], "gy": here[1], "gz": (here[2] + step) % line} for step in range(1, line)
     ]
-    moved_by = [[(here[k] + step) % counts[k] for step in range(counts[k])] for k in range(3)]
+    def others(k):
+        size = counts[k]
+        far_side = here[k] >= (size + 1) // 2
+        place = jnp.where(far_side, size - 1 - here[k], here[k])
+        steps = [(size - 1 - u, size - 1 - u) for u in range(size // 2)]
+        spots = [jnp.where(far_side, size - 1 - u, u) for u, _ in steps]
+        weights = [w for _, w in steps]
+        for step in range(1, size - size // 2):
+            u = (place + step) % (size - size // 2)
+            spots.append(jnp.where(far_side, size - 1 - u, u))
+            weights.append(0.5)
+        return list(zip(spots, weights)) + [(here[k], 0)]
+
+    moved_by = [others(k) for k in range(3)]
+    links = (0.5, 1.0, 1.0)
+    ranked = [
+        (sum(g * (m[1] > 0.5 or k > 0) * m[1] for k, (g, m) in enumerate(zip(links, spot))), n, spot)
+        for n, spot in enumerate(
+            (x, y, z) for x in moved_by[0] for y in moved_by[1] for z in moved_by[2]
+        )
+        if any(m[1] for m in spot)
+    ]
     all_targets = [
-        {"gx": moved_by[0][a], "gy": moved_by[1][b], "gz": moved_by[2][c]}
-        for c in reversed(range(counts[2]))
-        for b in reversed(range(counts[1]))
-        for a in reversed(range(counts[0]))
-        if a or b or c
+        {a: spot[k][0] for k, a in enumerate(AXES)}
+        for _, _, spot in sorted(ranked, key=lambda item: (-item[0], item[1]))
     ]
 
     regions = [r for r in REGIONS if abs(r[0]) < counts[0] and abs(r[1]) < counts[2]]
@@ -161,7 +199,7 @@
 
     def signal_all(semaphore):
         def act(steps):
-            for region in reversed(regions):
+            for region in sorted(regions, key=lambda r: (-abs(r[0]), -abs(r[1]))):
 
                 def go(region=region):
                     for way in ways_of(region, steps):
@@ -171,7 +209,13 @@
 
         by_class(act)
 
-    own = (pl.ds(depth, nx), pl.ds(0, ny), pl.ds(0, nz))
+    barrier = pltpu.get_barrier_semaphore()
+    signal_all(barrier)
+    if not direct:
+        for target in plane_targets + line_targets:
+            pl.semaphore_signal(barrier, inc=1, device_id=target, device_id_type=MESH)
+
+    own = (pl.ds(depth, nx), pl.ds(depth, ny))
     loads = [
         pltpu.make_async_copy(table_in, table_row, load_sems.at[0]),
         pltpu.make_async_copy(category_in, ints.at[0], load_sems.at[1]),
@@ -182,18 +226,12 @@
     for load in loads:
         load.start()
 
-    barrier = pltpu.get_barrier_semaphore()
-    signal_all(barrier)
-    if not direct:
-        for target in plane_targets + line_targets:
-            pl.semaphore_signal(barrier, inc=1, device_id=target, device_id_type=MESH)
-
     def clear(ref, *index):
         shape = ref.at[index].shape
         ref[index] = jnp.zeros(shape, jnp.float32)
 
     table[...] = jnp.zeros(table.shape, jnp.float32)
-    body = slice(0, nz)
+    everything = slice(None)
     for way, planes, slots in (
         ((-1, 0, 0), slice(0, depth), 0),
         ((1, 0, 0), slice(depth + nx, wide), 1 + BOTH),
@@ -202,42 +240,44 @@
         @pl.when(jnp.logical_not(exists(way)))
         def _():
             for f in range(2):
-                clear(pair, f, planes, slice(None), body)
-            clear(push_in, planes, slice(None), body)
-            clear(cool, planes, slice(None), body)
+                clear(pair, f, planes)
+            clear(push_in, planes)
+            clear(cool, planes)
             for side in range(2):
-                clear(beside, side, slots, slice(None), slice(None))
+                clear(beside, side, slots)
 
     for way, rows, few in (
-        ((0, 1, 0), slice(ny, ny + SUB), slice(ny, ny + SUB // 2)),
-        ((0, -1, 0), slice(tall - SUB, tall), slice(short - SUB // 2, short)),
+        ((0, 1, 0), slice(depth + ny, 2 * depth + ny), slice(ITERS + ny, short)),
+        ((0, -1, 0), slice(0, depth), slice(0, ITERS)),
     ):
 
         @pl.when(jnp.logical_not(exists(way)))
         def _():
             for f in range(2):
-                clear(pair, f, slice(None), rows, body)
-            clear(push_in, slice(None), few, body)
-            clear(cool, slice(None), few, body)
+                clear(pair, f, everything, rows)
+            clear(push_in, everything, few)
+            clear(cool, everything, few)
             for side in range(2):
-                clear(beside, side, slice(None), rows, slice(None))
+                clear(beside, side, everything, rows)
 
     for side, way in enumerate(((0, 0, -1), (0, 0, 1))):
 
         @pl.when(jnp.logical_not(exists(way)))
         def _():
-            clear(beside, side, slice(None), slice(None), slice(None))
-
-    def valid(index, size, cut, k):
-        inner = index < size
-        right = jnp.logical_and(index < size + cut, here[k] < counts[k] - 1)
-        left = jnp.logical_and(index >= size + cut, here[k] > 0)
-        return jnp.logical_or(inner, jnp.logical_or(right, left))
-
-    y_index = lax.broadcasted_iota(jnp.int32, (short, long), 0)
+            clear(beside, side)
+
+    row_index = lax.broadcasted_iota(jnp.int32, (short, long), 0)
+    y_index = leap * (row_index % SUB) + row_index // SUB - ITERS
     z_index = lax.broadcasted_iota(jnp.int32, (short, long), 1)
-    both_in = jnp.logical_and(valid(y_index, ny, SUB // 2, 1), valid(z_index, nz, LANES // 2, 2))
-    within = jnp.where(both_in, 1.0, 0.0)
+    y_low = jnp.logical_or(y_index >= 0, here[1] > 0)
+    y_high = jnp.logical_or(y_index < ny, here[1] < counts[1] - 1)
+    z_low = jnp.logical_or(z_index < nz + LANES // 2, here[2] > 0)
+    z_far = jnp.logical_or(z_index < nz, z_index >= nz + LANES // 2)
+    z_high = jnp.logical_or(z_far, here[2] < counts[2] - 1)
+    y_good, z_good = jnp.logical_and(y_low, y_high), jnp.logical_and(z_low, z_high)
+    within = jnp.where(jnp.logical_and(y_good, z_good), 1.0, 0.0)
+    y_own = jnp.logical_and(y_index >= 0, y_index < ny)[:, :nz]
+    row_mask[...] = jnp.where(y_own, 1.0, 0.0)
     masks[0] = jnp.where(here[0] > 0, 1.0, 0.0) * within
     masks[1] = within
     masks[2] = jnp.where(here[0] < counts[0] - 1, 1.0, 0.0) * within
@@ -262,12 +302,12 @@
     for i in range(nx):
         cond = jnp.take_along_axis(lookup, ints[0, i], axis=1)
         flag = ints[1, i].astype(jnp.float32)
-        warm = pair[0, depth + i, 0:ny, 0:nz]
+        warm = pair[0, depth + i, depth : depth + ny, :]
         push = interval_delta * source[i] - (interval_delta * cooling) * flag * warm
         push = twice * push
-        pair[1, depth + i, 0:ny, 0:nz] = cond
-        cool[depth + i, 0:ny, 0:nz] = flag
-        push_in[depth + i, 0:ny, 0:nz] = push
+        pair[1, depth + i, depth : depth + ny, :] = cond
+        cool[depth + i, ITERS : ITERS + ny, :] = flag
+        push_in[depth + i, ITERS : ITERS + ny, :] = push
         for g, start in enumerate((0, tail)):
             if not 0 <= i - start < depth:
                 continue
@@ -290,12 +330,12 @@
         waits = waits + (plane + line - 2)
     pl.semaphore_wait(barrier, waits)
 
-    def y_span(step, reach, full):
+    def y_span(step, reach, source_base, base):
         if step == 0:
-            return pl.ds(0, ny), pl.ds(0, ny)
+            return pl.ds(source_base, ny), pl.ds(base, ny)
         if step > 0:
-            return pl.ds(ny - reach, reach), pl.ds(full - reach, reach)
-        return pl.ds(0, reach), pl.ds(ny, reach)
+            return pl.ds(source_base + ny - reach, reach), pl.ds(base - reach, reach)
+        return pl.ds(source_base, reach), pl.ds(base + ny, reach)
 
     def x_span(step, reach):
         if step == 0:
@@ -314,21 +354,20 @@
             device_id_type=MESH,
         ).start()
 
-    def send_field(view, way, reach, full, stage):
+    def send_field(ref, way, reach, base, stage):
         src_x, dst_x = x_span(way[0], reach)
-        src_y, dst_y = y_span(way[1], reach, full)
-        z = pl.ds(0, nz)
-        send(view(src_x, src_y, z), view(dst_x, dst_y, z), way, stage)
+        src_y, dst_y = y_span(way[1], reach, base, base)
+        send(ref.at[src_x, src_y], ref.at[dst_x, dst_y], way, stage)
 
     def send_cond(way):
-        send_field(lambda *v: pair.at[(1,) + v], way, depth, tall, 0)
+        send_field(pair.at[1], way, depth, depth, 0)
 
     def send_warm(way):
-        send_field(lambda *v: pair.at[(0,) + v], way, depth, tall, 1)
+        send_field(pair.at[0], way, depth, depth, 1)
 
     def send_rest(way):
-        send_field(lambda *v: push_in.at[v], way, depth - 1, short, 2)
-        send_field(lambda *v: cool.at[v], way, depth - 2, short, 2)
+        send_field(push_in, way, depth - 1, ITERS, 2)
+        send_field(cool, way, depth - 2, ITERS, 2)
 
     def send_edges(way):
         if way[0] == 0:
@@ -337,7 +376,7 @@
             src_x, dst_x = pl.ds(1, 1), pl.ds(0, 1)
         else:
             src_x, dst_x = pl.ds(0, 1), pl.ds(1 + BOTH, 1)
-        src_y, dst_y = y_span(way[1], depth, tall)
+        src_y, dst_y = y_span(way[1], depth, 0, depth)
         side = 0 if way[2] > 0 else 1
         send(edges.at[side, src_x, src_y], beside.at[side, dst_x, dst_y], way, 0)
 
@@ -452,13 +491,7 @@
 
     wait_all((0, 3), halo_recv.at[0], True)
 
-    first_half = lax.broadcasted_iota(jnp.int32, (SUB, LANES), 0) < SUB // 2
     tall_lane = lax.broadcasted_iota(jnp.int32, (tall, LANES), 1)
-
-    def narrow(v):
-        mask = jnp.concatenate([first_half] * (v.shape[1] // LANES), axis=1)
-        join = jnp.where(mask, v[ny : ny + SUB], v[ny + SUB :])
-        return jnp.concatenate([v[:ny], join], axis=0)
 
     places = [(0, j) for j in range(depth)]
     places += [(1, p) if p < depth else (2, p - tail) for p in range(nx)]
@@ -466,22 +499,36 @@
 
     def unpack(fields):
         for i, (g, slot) in enumerate(places):
-            both = [beside[side, g] for side in range(2)]
-            if fields[0] >= 2:
-                both = [narrow(v) for v in both]
             for f in fields:
-                ref, spare = ((pair, 0), (pair, 0), (push_in, 1), (cool, 2))[f]
+                spare = (0, 0, 1, 2)[f]
                 if not spare <= i < wide - spare:
                     continue
                 cut = (slot * FIELDS + f + 1) * depth
-                kept = jnp.where(tall_lane[: both[0].shape[0]] < cut, both[0], both[1])
-                kept = pltpu.roll(kept, LANES - cut, 1)
                 if f < 2:
-                    ref[f, i, :, nz:] = kept
-                else:
-                    ref[i, :, nz:] = kept
+                    kept = jnp.where(tall_lane < cut, beside[0, g], beside[1, g])
+                    side_pair[f, i] = pltpu.roll(kept, LANES - cut, 1)
+                    continue
+                ref = side_push if f == 2 else side_cool
+                for t in range(leap):
+                    rows = pl.ds(1 + t, SUB, stride=leap)
+                    kept = jnp.where(tall_lane[:SUB] < cut, beside[0, g, rows, :], beside[1, g, rows, :])
+                    ref[i, t * SUB : (t + 1) * SUB, :] = pltpu.roll(kept, LANES - cut, 1)
 
     unpack((1, 0))
+
+    def pieces_of(f, i, first, some):
+        pieces = []
+        for j in range(first, first + some):
+            rows = pl.ds(j, SUB, stride=leap)
+            pieces.append(jnp.concatenate([pair[f, i, rows, :], side_pair[f, i, rows, :]], axis=1))
+        return pieces
+
+    def middle_of(f, i):
+        return jnp.concatenate(pieces_of(f, i, 1, leap), axis=0)
+
+    def joined(main, side, i):
+        rows = [main[i, pl.ds(t, SUB, stride=leap), :] for t in range(leap)]
+        return jnp.concatenate([jnp.concatenate(rows, axis=0), side[i]], axis=1)
 
     def along_x(least, most, planes_of, use):
         before = sums = None
@@ -495,42 +542,40 @@
             before = now
 
     def ring_of(i):
-        return (smooth_z(narrow(smooth_y(pair[1, i]))),)
+        return (smooth_z(smooth_rows(pieces_of(1, i, 0, leap + 2))),)
 
     def use_ring(i, ring):
-        cond = narrow(pair[1, i])
+        cond = middle_of(1, i)
         base = twice * (8.0 * interval_delta * cond + quarter * ring)
         spread[i] = base
         couple[i] = (quarter * twice) * cond
 
     along_x(0, wide, ring_of, use_ring)
+    unpack((2, 3))
 
     wait_all((1,), halo_recv.at[1], True)
 
     totals = [None] * MOMENTS
 
     def gather(n, a, b):
-        part = a * b
-        part = part[:SUB] + part[SUB:] if ny == 2 * SUB else sum(
-            part[r : r + SUB] for r in range(0, ny, SUB)
-        )
+        part = sum(tiles_of(a * b))
         totals[n] = part if totals[n] is None else totals[n] + part
 
     def core(v):
-        return v[:ny, :nz]
+        return v[:, :nz]
 
     def warm_of(i):
-        warm = pair[0, i]
-        warm_flux = (quarter * twice) * (pair[1, i] * warm)
-        return smooth_z(narrow(smooth_y(warm))), smooth_z(narrow(smooth_y(warm_flux)))
+        warm = pieces_of(0, i, 0, leap + 2)
+        cond = pieces_of(1, i, 0, leap + 2)
+        warm_flux = [(quarter * twice) * (a * b) for a, b in zip(warm, cond)]
+        return smooth_z(smooth_rows(warm)), smooth_z(smooth_rows(warm_flux))
 
     def use_warm(i, ring, push):
         edge = couple[i]
-        image = spread[i] * narrow(pair[0, i]) - (edge * ring + inside(i) * push)
+        image = spread[i] * middle_of(0, i) - (edge * ring + inside(i) * push)
         basis[0, i] = image
 
     along_x(0, wide, warm_of, use_warm)
-    unpack((2, 3))
 
     wait_all((2,), halo_recv.at[2], True)
 
@@ -539,17 +584,17 @@
         def level_of(i, k=k):
             mid = basis[k, i]
             if k == 0:
-                mid = push_in[i] - mid
+                mid = joined(push_in, side_push, i) - mid
                 basis[0, i] = mid
                 if depth <= i < depth + nx:
-                    gather(0, core(mid), core(mid))
+                    gather(0, row_mask[...] * core(mid), core(mid))
             return smooth_z(smooth_y(mid)), smooth_z(smooth_y(couple[i] * mid))
 
         def use_level(i, ring, push, k=k):
             edge = couple[i]
             mid = basis[k, i]
             if k == 0:
-                main = spread[i] + twice * ((1.0 - middle) + interval_delta * cooling * cool[i])
+                main = spread[i] + twice * ((1.0 - middle) + interval_delta * cooling * joined(cool, side_cool, i))
                 diag[i] = main
             else:
                 main = diag[i]
@@ -558,25 +603,24 @@
                 fresh = fresh - basis[k - 1, i]
             basis[k + 1, i] = fresh
             if depth <= i < depth + nx:
-                gather(2 * k + 1, core(mid), core(fresh))
-                gather(2 * k + 2, core(fresh), core(fresh))
+                kept = row_mask[...] * core(fresh)
+                gather(2 * k + 1, core(mid), kept)
+                gather(2 * k + 2, core(fresh), kept)
 
         along_x(k + 1, wide - k - 1, level_of, use_level)
 
     k = ITERS - 1
 
     def last_of(i):
-        return (
-            smooth_z_own(smooth_y(basis[k, i])[:ny]),
-            smooth_z_own(smooth_y(couple[i] * basis[k, i])[:ny]),
-        )
+        mid = basis[k, i]
+        return smooth_z_own(smooth_y(mid)), smooth_z_own(smooth_y(couple[i] * mid))
 
     def use_last(i, ring, push):
-        mid = basis[k, i, 0:ny, 0:nz]
-        fresh = diag[i, 0:ny, 0:nz] * mid - (couple[i, 0:ny, 0:nz] * ring + push)
-        fresh = fresh - basis[k - 1, i, 0:ny, 0:nz]
-        basis[k + 1, i, 0:ny, 0:nz] = fresh
-        gather(2 * k + 1, mid, fresh)
+        mid = core(basis[k, i])
+        fresh = core(diag[i]) * mid - (core(couple[i]) * ring + push)
+        fresh = fresh - core(basis[k - 1, i])
+        basis[k + 1, i, :, 0:nz] = fresh
+        gather(2 * k + 1, row_mask[...] * mid, fresh)
 
     along_x(depth - 1, depth + nx + 1, last_of, use_last)
 
@@ -593,6 +637,16 @@
 
     def settle():
         wait_all((0, 1, 2, 3), halo_send.at[0], False)
+        for n in range(ITERS + 1):
+            for i in range(nx):
+                for t in range(leap):
+                    tile = basis[n, depth + i, t * SUB : (t + 1) * SUB, 0:nz]
+                    natural[n, i, pl.ds(t, SUB, stride=leap), :] = tile
+        for n in range(ITERS + 1):
+            for i in range(nx):
+                natural_own[n, i] = natural[n, i, ITERS : ITERS + ny, :]
+        for i in range(nx):
+            natural_own[ITERS + 1, i] = pair[0, depth + i, depth : depth + ny, :]
 
     if direct:
         mine = in_plane * line + here[2]
@@ -666,10 +720,10 @@
             norm = following
 
     for i in range(nx):
-        warm = pair[0, depth + i, 0:ny, 0:nz]
+        warm = natural_own[ITERS + 1, i]
         end = jnp.zeros_like(warm)
         for k in range(ITERS + 1):
-            value = basis[k, depth + i, 0:ny, 0:nz]
+            value = natural_own[k, i]
             if k < ITERS:
                 warm = warm + moved[k] * value
             end = end + left[k] * value
@@ -696,14 +750,20 @@
         in_specs=[any_spec] * 5,
         out_specs=vmem,
         scratch_shapes=[
-            pltpu.VMEM((2, wide, tall, long), f32),
-            pltpu.VMEM((wide, short, long), f32),
-            pltpu.VMEM((wide, short, long), f32),
+            pltpu.VMEM((2, wide, tall, nz), f32),
+            pltpu.VMEM((2, wide, tall, nz), f32),
+            pltpu.VMEM((wide, short, nz), f32),
+            pltpu.VMEM((wide, short, nz), f32),
+            pltpu.VMEM((wide, short, nz), f32),
+            pltpu.VMEM((wide, short, nz), f32),
             pltpu.VMEM((ITERS + 1, wide, short, long), f32),
             pltpu.VMEM((wide, short, long), f32),
             pltpu.VMEM((wide, short, long), f32),
             pltpu.VMEM((wide, short, long), f32),
             pltpu.VMEM((3, short, long), f32),
+            pltpu.VMEM((short, nz), f32),
+            pltpu.VMEM((ITERS + 1, nx, short, nz), f32),
+            pltpu.VMEM((ITERS + 2, nx, ny, nz), f32),
             pltpu.VMEM((SUB, LANES), f32),
             pltpu.VMEM(table.shape, f32),
             pltpu.VMEM((nx, ny, nz), f32),

time: 18.1 us -> 17.8 us (0.983)
  Pallas kernels: 16.6 us -> 16.3 us
    pallas_call x1, Pallas kernels: 16.6 us -> 16.3 us  [body(): pl.pallas_call(functools.partial(kernel, counts), out_shape=pltpu.VMEM((2...]
where the time goes in v5:
time: 17.8 us; the launch traced here: 17.6 us
  Pallas kernels  16.3 us (92%)
  local copies, waits for them, and re-layouts  0.66 us (4%)
  between operations  0.64 us (4%)
    pallas_call x1, Pallas kernels, body(): pl.pallas_call(functools.partial(kernel, counts), out_shape=pltpu.VMEM((2...  16.3 us
    squeeze x1, local copies, waits for them, and re-layouts, body(): return (both[0], both[1])  0.66 us

profile of v5, /device:TPU:0, one launch (start us, length us, event | category | flops | bytes accessed | tf_op | source)
XLA Modules:
  0.0 17.6 jit_solution(16778729426199079543)
XLA Ops:
  0.6 16.3 %shard_map.68 = f32[2,8,16,128]{3,2,1,0:T(8,128)S(1)} custom-call(f32[8,16,128]{2,1,0:T(8,128)} %warm_in.1, f32[8,16,128]{2,1,0:T(8,128)} %source_in.1, s32[8,16,128]{2,1,0:T(8,128)} %category_in.1, f32[1,16]{1,0:T(1,128)} %bitcast.5, s32[8,16,128]{2,1,0:T(8,128)} %flags_in.1), custom_call_target="tpu_custom_call" | custom-call | tf_op jit(solution)/shard_map/pallas_call | solution.py:747
  17.0 0.7 %slice_bitcast_fusion = (f32[8,16,128]{2,1,0:T(8,128)}, f32[8,16,128]{2,1,0:T(8,128)}) fusion(f32[2,8,16,128]{3,2,1,0:T(8,128)S(1)} %shard_map.68), kind=kLoop, calls=%fused_computation | loop fusion | bytes 262144 | tf_op jit(solution)/shard_map/squeeze | solution.py:788

commit v6 on v5

--- a/solution.py
+++ b/solution.py
@@ -40,18 +40,28 @@
     return jnp.concatenate([a + b for a, b in zip(pairs, pairs[1:])], axis=0)
 
 
-def smooth_z(values):
-    size = values.shape[1]
-    return (values + values) + (pltpu.roll(values, 1, 1) + pltpu.roll(values, size - 1, 1))
-
-
-def smooth_z_own(values):
+def beside_z(values):
+    return pltpu.roll(values, 1, 1), pltpu.roll(values, values.shape[1] - 1, 1)
+
+
+def beside_z_own(values):
     size = values.shape[1] // 2
     main, side = values[:, :size], values[:, size:]
     lane = lax.broadcasted_iota(jnp.int32, main.shape, 1)
     before = pltpu.roll(jnp.where(lane == size - 1, side, main), 1, 1)
-    after = pltpu.roll(jnp.where(lane == 0, side, main), size - 1, 1)
-    return (main + main) + (before + after)
+    return before, pltpu.roll(jnp.where(lane == 0, side, main), size - 1, 1)
+
+
+def smooth_z(values):
+    before, after = beside_z(values)
+    return (values + values) + (before + after)
+
+
+def sums_z(values, around, edges):
+    before, after = around
+    twice = values + values
+    own = twice + (before + after)
+    return own, edges[0] * twice + (edges[1] * before + edges[2] * after)
 
 
 def kernel(
@@ -71,7 +81,7 @@
     basis,
     spread,
     diag,
-    couple,
+    couples,
     masks,
     row_mask,
     natural,
@@ -542,13 +552,14 @@
             before = now
 
     def ring_of(i):
-        return (smooth_z(smooth_rows(pieces_of(1, i, 0, leap + 2))),)
+        edge = (quarter * twice) * jnp.concatenate(pieces_of(1, i, 0, leap + 2), axis=0)
+        before, after = beside_z(edge)
+        for n, value in enumerate((edge, before, after)):
+            couples[n, i] = value[SUB : SUB + short]
+        return (smooth_rows(tiles_of((edge + edge) + (before + after))),)
 
     def use_ring(i, ring):
-        cond = middle_of(1, i)
-        base = twice * (8.0 * interval_delta * cond + quarter * ring)
-        spread[i] = base
-        couple[i] = (quarter * twice) * cond
+        spread[i] = (8.0 * interval_delta / quarter) * couples[0, i] + ring
 
     along_x(0, wide, ring_of, use_ring)
     unpack((2, 3))
@@ -571,7 +582,7 @@
         return smooth_z(smooth_rows(warm)), smooth_z(smooth_rows(warm_flux))
 
     def use_warm(i, ring, push):
-        edge = couple[i]
+        edge = couples[0, i]
         image = spread[i] * middle_of(0, i) - (edge * ring + inside(i) * push)
         basis[0, i] = image
 
@@ -588,10 +599,11 @@
                 basis[0, i] = mid
                 if depth <= i < depth + nx:
                     gather(0, row_mask[...] * core(mid), core(mid))
-            return smooth_z(smooth_y(mid)), smooth_z(smooth_y(couple[i] * mid))
+            sums = sums_z(mid, beside_z(mid), [couples[n, i] for n in range(3)])
+            return [smooth_y(value) for value in sums]
 
         def use_level(i, ring, push, k=k):
-            edge = couple[i]
+            edge = couples[0, i]
             mid = basis[k, i]
             if k == 0:
                 main = spread[i] + twice * ((1.0 - middle) + interval_delta * cooling * joined(cool, side_cool, i))
@@ -613,11 +625,13 @@
 
     def last_of(i):
         mid = basis[k, i]
-        return smooth_z_own(smooth_y(mid)), smooth_z_own(smooth_y(couple[i] * mid))
+        edges_own = [core(couples[n, i]) for n in range(3)]
+        sums = sums_z(core(mid), beside_z_own(mid), edges_own)
+        return [smooth_y(value) for value in sums]
 
     def use_last(i, ring, push):
         mid = core(basis[k, i])
-        fresh = core(diag[i]) * mid - (core(couple[i]) * ring + push)
+        fresh = core(diag[i]) * mid - (core(couples[0, i]) * ring + push)
         fresh = fresh - core(basis[k - 1, i])
         basis[k + 1, i, :, 0:nz] = fresh
         gather(2 * k + 1, row_mask[...] * mid, fresh)
@@ -759,7 +773,7 @@
             pltpu.VMEM((ITERS + 1, wide, short, long), f32),
             pltpu.VMEM((wide, short, long), f32),
             pltpu.VMEM((wide, short, long), f32),
-            pltpu.VMEM((wide, short, long), f32),
+            pltpu.VMEM((3, wide, short, long), f32),
             pltpu.VMEM((3, short, long), f32),
             pltpu.VMEM((short, nz), f32),
             pltpu.VMEM((ITERS + 1, nx, short, nz), f32),

time: 17.8 us -> 17.7 us (level)
  no operation moved by 1% of the time
where the time goes in v6:
time: 17.7 us; the launch traced here: 17.6 us
  Pallas kernels  16.3 us (92%)
  local copies, waits for them, and re-layouts  0.66 us (4%)
  between operations  0.64 us (4%)
    pallas_call x1, Pallas kernels, body(): pl.pallas_call(functools.partial(kernel, counts), out_shape=pltpu.VMEM((2...  16.3 us
    squeeze x1, local copies, waits for them, and re-layouts, body(): return (both[0], both[1])  0.66 us

profile of v6, /device:TPU:0, one launch (start us, length us, event | category | flops | bytes accessed | tf_op | source)
XLA Modules:
  0.0 17.6 jit_solution(14094776465898871232)
XLA Ops:
  0.6 16.3 %shard_map.68 = f32[2,8,16,128]{3,2,1,0:T(8,128)S(1)} custom-call(f32[8,16,128]{2,1,0:T(8,128)} %warm_in.1, f32[8,16,128]{2,1,0:T(8,128)} %source_in.1, s32[8,16,128]{2,1,0:T(8,128)} %category_in.1, f32[1,16]{1,0:T(1,128)} %bitcast.5, s32[8,16,128]{2,1,0:T(8,128)} %flags_in.1), custom_call_target="tpu_custom_call" | custom-call | tf_op jit(solution)/shard_map/pallas_call | solution.py:761
  16.9 0.7 %slice_bitcast_fusion = (f32[8,16,128]{2,1,0:T(8,128)}, f32[8,16,128]{2,1,0:T(8,128)}) fusion(f32[2,8,16,128]{3,2,1,0:T(8,128)S(1)} %shard_map.68), kind=kLoop, calls=%fused_computation | loop fusion | bytes 262144 | tf_op jit(solution)/shard_map/squeeze | solution.py:802

commit v7 on v6

--- a/solution.py
+++ b/solution.py
@@ -55,6 +55,17 @@
 def smooth_z(values):
     before, after = beside_z(values)
     return (values + values) + (before + after)
+
+
+def smooth_z_two(first, second, bands):
+    rows = first.shape[0]
+    both = jnp.concatenate([first, second], axis=0)
+    coarse = both.astype(jnp.bfloat16)
+    fine = (both - coarse.astype(jnp.float32)).astype(jnp.bfloat16)
+    parts = jnp.concatenate([coarse, fine], axis=0)
+    sums = jnp.dot(parts, bands[...], preferred_element_type=jnp.float32)
+    sums = sums[: 2 * rows] + sums[2 * rows :]
+    return sums[:rows], sums[rows:]
 
 
 def sums_z(values, around, edges):
@@ -84,6 +95,7 @@
     couples,
     masks,
     row_mask,
+    bands,
     natural,
     natural_own,
     table,
@@ -295,6 +307,12 @@
     def inside(i):
         return masks[0 if i < depth else 2 if i >= depth + nx else 1]
 
+    from_lane = lax.broadcasted_iota(jnp.int32, (long, long), 0)
+    to_lane = lax.broadcasted_iota(jnp.int32, (long, long), 1)
+    gap = jnp.abs(from_lane - to_lane)
+    near_lane = jnp.logical_or(gap == 1, gap == long - 1)
+    bands[...] = jnp.where(gap == 0, 2.0, jnp.where(near_lane, 1.0, 0.0)).astype(jnp.bfloat16)
+
     loads[0].wait()
     table[0:1, 0 : table_in.shape[1]] = table_row[...]
     most = 7.0 + 24.0 * jnp.max(table[0:1, :], axis=1, keepdims=True)
@@ -575,11 +593,17 @@
     def core(v):
         return v[:, :nz]
 
-    def warm_of(i):
+    pushes = {}
+
+    def flux_rows(i):
         warm = pieces_of(0, i, 0, leap + 2)
         cond = pieces_of(1, i, 0, leap + 2)
-        warm_flux = [(quarter * twice) * (a * b) for a, b in zip(warm, cond)]
-        return smooth_z(smooth_rows(warm)), smooth_z(smooth_rows(warm_flux))
+        return smooth_rows([(quarter * twice) * (a * b) for a, b in zip(warm, cond)])
+
+    def warm_of(i):
+        if i % 2 == 0:
+            pushes[i], pushes[i + 1] = smooth_z_two(flux_rows(i), flux_rows(i + 1), bands)
+        return smooth_z(smooth_rows(pieces_of(0, i, 0, leap + 2))), pushes.pop(i)
 
     def use_warm(i, ring, push):
         edge = couples[0, i]
@@ -776,6 +800,7 @@
             pltpu.VMEM((3, wide, short, long), f32),
             pltpu.VMEM((3, short, long), f32),
             pltpu.VMEM((short, nz), f32),
+            pltpu.VMEM((long, long), jnp.bfloat16),
             pltpu.VMEM((ITERS + 1, nx, short, nz), f32),
             pltpu.VMEM((ITERS + 2, nx, ny, nz), f32),
             pltpu.VMEM((SUB, LANES), f32),

time: 17.7 us -> 17.7 us (level)
  no operation moved by 1% of the time
where the time goes in v7:
time: 17.7 us; the launch traced here: 17.5 us
  Pallas kernels  16.2 us (92%)
  local copies, waits for them, and re-layouts  0.66 us (4%)
  between operations  0.64 us (4%)
    pallas_call x1, Pallas kernels, body(): pl.pallas_call(functools.partial(kernel, counts), out_shape=pltpu.VMEM((2...  16.2 us
    squeeze x1, local copies, waits for them, and re-layouts, body(): return (both[0], both[1])  0.66 us

profile of v7, /device:TPU:0, one launch (start us, length us, event | category | flops | bytes accessed | tf_op | source)
XLA Modules:
  0.0 17.5 jit_solution(12906644798610721831)
XLA Ops:
  0.6 16.2 %shard_map.68 = f32[2,8,16,128]{3,2,1,0:T(8,128)S(1)} custom-call(f32[8,16,128]{2,1,0:T(8,128)} %warm_in.1, f32[8,16,128]{2,1,0:T(8,128)} %source_in.1, s32[8,16,128]{2,1,0:T(8,128)} %category_in.1, f32[1,16]{1,0:T(1,128)} %bitcast.5, s32[8,16,128]{2,1,0:T(8,128)} %flags_in.1), custom_call_target="tpu_custom_call" | custom-call | tf_op jit(solution)/shard_map/pallas_call | solution.py:785
  16.9 0.7 %slice_bitcast_fusion = (f32[8,16,128]{2,1,0:T(8,128)}, f32[8,16,128]{2,1,0:T(8,128)}) fusion(f32[2,8,16,128]{3,2,1,0:T(8,128)S(1)} %shard_map.68), kind=kLoop, calls=%fused_computation | loop fusion | bytes 262144 | tf_op jit(solution)/shard_map/squeeze | solution.py:827

commit v8 on v7

--- a/solution.py
+++ b/solution.py
@@ -108,6 +108,8 @@
     row_out,
     plane_rows,
     line_rows,
+    plane_bounds,
+    line_bounds,
     all_rows,
     load_sems,
     halo_send,
@@ -233,9 +235,8 @@
 
     barrier = pltpu.get_barrier_semaphore()
     signal_all(barrier)
-    if not direct:
-        for target in plane_targets + line_targets:
-            pl.semaphore_signal(barrier, inc=1, device_id=target, device_id_type=MESH)
+    for target in plane_targets + line_targets:
+        pl.semaphore_signal(barrier, inc=1, device_id=target, device_id_type=MESH)
 
     own = (pl.ds(depth, nx), pl.ds(depth, ny))
     loads = [
@@ -315,11 +316,6 @@
 
     loads[0].wait()
     table[0:1, 0 : table_in.shape[1]] = table_row[...]
-    most = 7.0 + 24.0 * jnp.max(table[0:1, :], axis=1, keepdims=True)
-    high, low = most, jnp.ones_like(most)
-    middle = 0.5 * (high + low)
-    half = 0.5 * (high - low)
-    twice = 2.0 / half
     quarter = 0.125 * interval_delta
     lookup = jnp.broadcast_to(table[0:1, :], (ny, LANES))
     lane = lax.broadcasted_iota(jnp.int32, (ny, LANES), 1)
@@ -332,7 +328,9 @@
         flag = ints[1, i].astype(jnp.float32)
         warm = pair[0, depth + i, depth : depth + ny, :]
         push = interval_delta * source[i] - (interval_delta * cooling) * flag * warm
-        push = twice * push
+        tops = (cond, cond, flag, flag) if i == 0 else (
+            jnp.maximum(tops[0], cond), tops[1] + cond, jnp.maximum(tops[2], flag), jnp.minimum(tops[3], flag)
+        )
         pair[1, depth + i, depth : depth + ny, :] = cond
         cool[depth + i, ITERS : ITERS + ny, :] = flag
         push_in[depth + i, ITERS : ITERS + ny, :] = push
@@ -353,10 +351,45 @@
         for g in range(BOTH):
             edges[side, g] = packed[side][g]
 
+    shrink = lambda op, v: op(op(v, axis=0, keepdims=True), axis=1, keepdims=True)
+    mean = shrink(jnp.sum, tops[1]) * (1.0 / (nx * ny * nz))
+    high = 1.0 + interval_delta * cooling * shrink(jnp.max, tops[2])
+    high = high + 8.0 * interval_delta * (shrink(jnp.max, tops[0]) + mean)
+    low = 1.0 + interval_delta * cooling * shrink(jnp.min, tops[3])
+    row_lane = lax.broadcasted_iota(jnp.int32, (1, LANES), 1)
+    bound = jnp.where(row_lane == 0, high, -low)
+    row_out[2] = bound
+    plane_bounds[in_plane] = bound
+
     waits = neighbours()
-    if not direct:
-        waits = waits + (plane + line - 2)
+    waits = waits + (plane + line - 2)
     pl.semaphore_wait(barrier, waits)
+
+    def share(stage, rows_ref, slot, targets):
+        for target in targets:
+            pltpu.make_async_remote_copy(
+                src_ref=row_out.at[stage],
+                dst_ref=rows_ref.at[slot],
+                send_sem=row_send.at[stage],
+                recv_sem=row_recv.at[stage],
+                device_id=target,
+                device_id_type=MESH,
+            ).start()
+
+    def share_wait(stage, rows_ref, targets):
+        if targets:
+            whole = pltpu.make_async_remote_copy(
+                src_ref=rows_ref.at[pl.ds(0, len(targets))],
+                dst_ref=rows_ref.at[pl.ds(0, len(targets))],
+                send_sem=row_send.at[stage],
+                recv_sem=row_recv.at[stage],
+                device_id=targets[0],
+                device_id_type=MESH,
+            )
+            whole.wait_send()
+            whole.wait_recv()
+
+    share(2, plane_bounds, in_plane, plane_targets)
 
     def y_span(step, reach, source_base, base):
         if step == 0:
@@ -493,29 +526,11 @@
         for hop in hops:
             signal(far, hop)
 
-    def share(stage, rows_ref, slot, targets):
-        for target in targets:
-            pltpu.make_async_remote_copy(
-                src_ref=row_out.at[stage],
-                dst_ref=rows_ref.at[slot],
-                send_sem=row_send.at[stage],
-                recv_sem=row_recv.at[stage],
-                device_id=target,
-                device_id_type=MESH,
-            ).start()
-
-    def share_wait(stage, rows_ref, targets):
-        if targets:
-            whole = pltpu.make_async_remote_copy(
-                src_ref=rows_ref.at[pl.ds(0, len(targets))],
-                dst_ref=rows_ref.at[pl.ds(0, len(targets))],
-                send_sem=row_send.at[stage],
-                recv_sem=row_recv.at[stage],
-                device_id=targets[0],
-                device_id_type=MESH,
-            )
-            whole.wait_send()
-            whole.wait_recv()
+    share_wait(2, plane_bounds, plane_targets)
+    bound = jnp.max(plane_bounds[...], axis=0)
+    row_out[3] = bound
+    line_bounds[here[2]] = bound
+    share(3, line_bounds, here[2], line_targets)
 
     wait_all((0, 3), halo_recv.at[0], True)
 
@@ -570,7 +585,7 @@
             before = now
 
     def ring_of(i):
-        edge = (quarter * twice) * jnp.concatenate(pieces_of(1, i, 0, leap + 2), axis=0)
+        edge = quarter * jnp.concatenate(pieces_of(1, i, 0, leap + 2), axis=0)
         before, after = beside_z(edge)
         for n, value in enumerate((edge, before, after)):
             couples[n, i] = value[SUB : SUB + short]
@@ -598,7 +613,7 @@
     def flux_rows(i):
         warm = pieces_of(0, i, 0, leap + 2)
         cond = pieces_of(1, i, 0, leap + 2)
-        return smooth_rows([(quarter * twice) * (a * b) for a, b in zip(warm, cond)])
+        return smooth_rows([quarter * (a * b) for a, b in zip(warm, cond)])
 
     def warm_of(i):
         if i % 2 == 0:
@@ -613,6 +628,14 @@
     along_x(0, wide, warm_of, use_warm)
 
     wait_all((2,), halo_recv.at[2], True)
+
+    share_wait(3, line_bounds, line_targets)
+    bound = jnp.max(line_bounds[...], axis=0)
+    pick_one = lambda v, n: jnp.sum(jnp.where(row_lane == n, v, 0.0), axis=1, keepdims=True)
+    high, low = pick_one(bound, 0), -pick_one(bound, 1)
+    middle = 0.5 * (high + low)
+    half = 0.5 * (high - low)
+    twice = 2.0 / half
 
     for k in range(ITERS - 1):
 
@@ -630,11 +653,11 @@
             edge = couples[0, i]
             mid = basis[k, i]
             if k == 0:
-                main = spread[i] + twice * ((1.0 - middle) + interval_delta * cooling * joined(cool, side_cool, i))
+                main = spread[i] + ((1.0 - middle) + interval_delta * cooling * joined(cool, side_cool, i))
                 diag[i] = main
             else:
                 main = diag[i]
-            fresh = main * mid - (edge * ring + inside(i) * push)
+            fresh = twice * (main * mid - (edge * ring + inside(i) * push))
             if k > 0:
                 fresh = fresh - basis[k - 1, i]
             basis[k + 1, i] = fresh
@@ -655,7 +678,7 @@
 
     def use_last(i, ring, push):
         mid = core(basis[k, i])
-        fresh = core(diag[i]) * mid - (core(couples[0, i]) * ring + push)
+        fresh = twice * (core(diag[i]) * mid - (core(couples[0, i]) * ring + push))
         fresh = fresh - core(basis[k - 1, i])
         basis[k + 1, i, :, 0:nz] = fresh
         gather(2 * k + 1, row_mask[...] * mid, fresh)
@@ -738,7 +761,7 @@
             value = inner if value is None else value + inner
         return value
 
-    left = [0.5 * half]
+    left = [jnp.ones_like(half)]
     heading = list(left)
     moved = []
     norm = product(left, left)
@@ -810,15 +833,17 @@
             pltpu.VMEM((2, BOTH, ny, nz), f32),
             pltpu.VMEM((2, BOTH + 2, tall, nz), f32),
             pltpu.VMEM((16 * nx * ny, LANES), f32),
-            pltpu.VMEM((2, 1, LANES), f32),
+            pltpu.VMEM((4, 1, LANES), f32),
+            pltpu.VMEM((plane, 1, LANES), f32),
+            pltpu.VMEM((line, 1, LANES), f32),
             pltpu.VMEM((plane, 1, LANES), f32),
             pltpu.VMEM((line, 1, LANES), f32),
             pltpu.VMEM((plane * line, 1, LANES), f32),
             pltpu.SemaphoreType.DMA((2,)),
             pltpu.SemaphoreType.DMA((1,)),
             pltpu.SemaphoreType.DMA((3,)),
-            pltpu.SemaphoreType.DMA((2,)),
-            pltpu.SemaphoreType.DMA((2,)),
+            pltpu.SemaphoreType.DMA((4,)),
+            pltpu.SemaphoreType.DMA((4,)),
             pltpu.SemaphoreType.REGULAR,
             pltpu.SemaphoreType.REGULAR,
         ],

time: 17.7 us -> 19.5 us (1.10)
  Pallas kernels: 16.2 us -> 18 us
    pallas_call x1, Pallas kernels: 16.2 us -> 18 us  [body(): pl.pallas_call(functools.partial(kernel, counts), out_shape=pltpu.VMEM((2...]
where the time goes in v8:
time: 19.5 us; the launch traced here: 19.3 us
  Pallas kernels  18 us (92%)
  local copies, waits for them, and re-layouts  0.66 us (3%)
  between operations  0.64 us (3%)
    pallas_call x1, Pallas kernels, body(): pl.pallas_call(functools.partial(kernel, counts), out_shape=pltpu.VMEM((2...  18 us
    squeeze x1, local copies, waits for them, and re-layouts, body(): return (both[0], both[1])  0.66 us

profile of v8, /device:TPU:0, one launch (start us, length us, event | category | flops | bytes accessed | tf_op | source)
XLA Modules:
  0.0 19.3 jit_solution(1314680416483343295)
XLA Ops:
  0.6 18.0 %shard_map.68 = f32[2,8,16,128]{3,2,1,0:T(8,128)S(1)} custom-call(f32[8,16,128]{2,1,0:T(8,128)} %warm_in.1, f32[8,16,128]{2,1,0:T(8,128)} %source_in.1, s32[8,16,128]{2,1,0:T(8,128)} %category_in.1, f32[1,16]{1,0:T(1,128)} %bitcast.5, s32[8,16,128]{2,1,0:T(8,128)} %flags_in.1), custom_call_target="tpu_custom_call" | custom-call | tf_op jit(solution)/shard_map/pallas_call | solution.py:808
  18.7 0.7 %slice_bitcast_fusion = (f32[8,16,128]{2,1,0:T(8,128)}, f32[8,16,128]{2,1,0:T(8,128)}) fusion(f32[2,8,16,128]{3,2,1,0:T(8,128)S(1)} %shard_map.68), kind=kLoop, calls=%fused_computation | loop fusion | bytes 262144 | tf_op jit(solution)/shard_map/squeeze | solution.py:852
